TPU v7x, 256 devices: a whole 4x4x8 slice. The times are simulated.
256 devices in a mesh: grp: 8 (over x, core), lat: 32 (over y, z).
Axes of the slice: x: 4, y: 4, z: 8, core: 2. Of those that a mesh axis runs over, the one named last changes fastest.
Arguments:
- grid_state: bfloat16 [32, 192, 384, 128], P('grp', 'lat'), may hold values from -6 to 6
- noise_field: bfloat16 [32, 192, 384, 128], P('grp', 'lat'), may hold values from -6 to 6
- legendre: bfloat16 [192, 128, 128], P('lat'), may hold values from -0.4375 to 0.4375
- diffusion: float32 [128], replicated, may hold values from 0.1 to 10
- input_weight: bfloat16 [128, 256], replicated, may hold values from -0.5 to 0.5
- noise_weight: bfloat16 [128, 256], replicated, may hold values from -0.5 to 0.5
- input_bias: float32 [256], replicated, may hold values from -4 to 4
- middle_weight: bfloat16 [256, 256], replicated, may hold values from -0.375 to 0.375
- output_weight: bfloat16 [256, 128], replicated, may hold values from -0.375 to 0.375
Outputs:
- new_state: bfloat16 [32, 192, 384, 128], P('grp', 'lat')
- ens_mean: float32 [192, 384, 128], P('lat')
- ens_var: float32 [192, 384, 128], P('lat')
All inputs are finite; a program needn't handle non-finite values.
Results may differ from a plain program's by a relative error of at most 0.012.
Values may be sent and summed in bfloat16 or wider, within the bound.
A program may use at most 128 MiB of HBM per device.

v0:
```python
import math

import jax
import jax.numpy as jnp
from jax import lax
from jax.sharding import PartitionSpec as P


def total_of_pieces(x, axis):
    return lax.all_gather(x, axis).astype(jnp.float32).sum(0)


def wave_table(lon_count, wave_count):
    lon_ids = jnp.arange(lon_count, dtype=jnp.int32)[:, None]
    wave_ids = jnp.arange(wave_count, dtype=jnp.int32)[None, :]
    phase = (lon_ids * wave_ids % lon_count).astype(jnp.float32) * (2.0 * math.pi / lon_count)
    factor = math.sqrt(2.0 / lon_count)
    joined = jnp.concatenate([jnp.cos(phase), -jnp.sin(phase)], axis=1) * factor
    return joined.astype(jnp.bfloat16)


def damping_filter(diffusion, wave_count):
    degree = jnp.arange(wave_count, dtype=jnp.int32).astype(jnp.float32)
    ratio = degree * (degree + 1.0) / float((wave_count - 1) * wave_count)
    return 1.0 / (1.0 + diffusion[None, :] * (ratio * ratio)[:, None])


def per_device(
    grid_state,
    noise_field,
    legendre,
    diffusion,
    input_weight,
    noise_weight,
    input_bias,
    middle_weight,
    output_weight,
):
    members, lat_rows, lon_count, channels = grid_state.shape
    wave_count = legendre.shape[1]
    local_waves = wave_count // lax.axis_size("lat")
    transform = wave_table(lon_count, wave_count)
    fourier = jnp.einsum(
        "blxc,xk->blkc", grid_state, transform, preferred_element_type=jnp.float32
    ).astype(jnp.bfloat16)
    fourier = fourier.reshape(members, lat_rows, 2, wave_count, channels)
    basis_band = lax.all_to_all(legendre, "lat", split_axis=1, concat_axis=0, tiled=True)
    zonal_ids = lax.axis_index("lat") * local_waves + jnp.arange(local_waves, dtype=jnp.int32)
    total_ids = jnp.arange(wave_count, dtype=jnp.int32)
    triangle = (total_ids[None, :] >= zonal_ids[:, None]).astype(jnp.float32)
    damping = damping_filter(diffusion, wave_count)
    spectrum = jnp.einsum(
        "lmn,blrmc->brmnc",
        basis_band,
        lax.all_to_all(fourier, "lat", split_axis=3, concat_axis=1, tiled=True),
        preferred_element_type=jnp.float32,
    )
    spectrum = spectrum * triangle[None, None, :, :, None]
    filtered = (spectrum * damping[None, None, None, :, :]).astype(jnp.bfloat16)
    banded_grid = jnp.einsum(
        "lmn,brmnc->blrmc", basis_band, filtered, preferred_element_type=jnp.float32
    ).astype(jnp.bfloat16)
    grid_fourier = lax.all_to_all(banded_grid, "lat", split_axis=1, concat_axis=3, tiled=True)
    grid_fourier = grid_fourier.reshape(members, lat_rows, 2 * wave_count, channels)
    smoothed = jnp.einsum(
        "bljc,xj->blxc", grid_fourier, transform, preferred_element_type=jnp.float32
    )
    flat_fields = smoothed.reshape(-1, channels)
    smoothed_in = flat_fields.astype(jnp.bfloat16)
    pre_act = jnp.dot(smoothed_in, input_weight, preferred_element_type=jnp.float32)
    pre_act = pre_act + jnp.dot(
        noise_field.reshape(-1, noise_field.shape[3]),
        noise_weight,
        preferred_element_type=jnp.float32,
    )
    hidden_one = jax.nn.silu(pre_act + input_bias).astype(jnp.bfloat16)
    hidden_two = jax.nn.silu(
        jnp.dot(hidden_one, middle_weight, preferred_element_type=jnp.float32)
    ).astype(jnp.bfloat16)
    tendency = jnp.dot(hidden_two, output_weight, preferred_element_type=jnp.float32)
    new_state = (flat_fields + tendency).astype(jnp.bfloat16).reshape(grid_state.shape)
    member_values = new_state.astype(jnp.float32)
    ensemble = members * lax.axis_size("grp")
    summed = total_of_pieces(jnp.sum(member_values, axis=0).astype(jnp.bfloat16), "grp").astype(
        jnp.float32
    )
    ens_mean = summed / ensemble
    spread = total_of_pieces(
        jnp.sum(jnp.square(member_values - ens_mean), axis=0).astype(jnp.bfloat16), "grp"
    ).astype(jnp.float32)
    ens_var = spread / (ensemble - 1)
    return (new_state, ens_mean, ens_var)


def solution(mesh):
    in_specs = (
        P("grp", "lat", None, None),
        P("grp", "lat", None, None),
        P("lat", None, None),
        P(),
        P(),
        P(),
        P(),
        P(),
        P(),
    )
    out_specs = (P("grp", "lat", None, None), P("lat", None, None), P("lat", None, None))
    return jax.shard_map(
        per_device, mesh=mesh, in_specs=in_specs, out_specs=out_specs, check_vma=False
    )
```

profile of v0, /device:TPU:1, one launch (start us, length us, event | category | flops | bytes accessed | tf_op | source)
XLA Modules:
  0.0 250.5 jit_solution(15547846299608432745)
XLA Ops:
  7.2 0.0 copy-start
  7.2 1.9 copy.32
  9.1 12.0 %all-to-all-start.1 = ((bf16[6,128,128]{2,0,1:T(8,128)(2,1)}), bf16[6,128,128]{2,0,1:T(8,128)(2,1)S(1)}, u32[]{:S(2)}, u32[]{:S(2)}) async-start(bf16[6,128,128]{2,0,1:T(8,128)(2,1)} %copy.32), calls=%async_computation.1 | async-start | bytes 524288 | tf_op jit(solution)/shard_map/all_to_all | solution.py:47
  21.1 0.8 sine_negate_fusion
  21.9 2.6 %convolution_convert_fusion = bf16[256,4,6,128]{3,0,2,1:T(8,128)(2,1)S(1)} fusion(bf16[4,6,384,128]{3,2,1,0:T(8,128)(2,1)} %param.9, f32[384,128]{0,1:T(8,128)S(1)} %get-tuple-element.3, f32[384,128]{0,1:T(8,128)S(1)} %get-tuple-element.4), kind=kOutput, calls=%fused_computation.13 | convolution fusion | flops 605061120 | bytes 4325376 | tf_op jit(solution)/shard_map/blxc,xk->blkc/dot_general | solution.py:43
  24.6 2.8 %copy.29 = bf16[4,6,2,128,128]{4,2,1,0,3:T(2,128)(2,1)} copy(bf16[4,6,2,128,128]{4,3,2,1,0:T(8,128)(2,1)S(1)} %bitcast.58) | data formatting | bytes 3145728 | tf_op jit(solution)/shard_map/reshape | solution.py:46
  27.4 0.0 copy-start.5
  27.4 3.5 %all-to-all-done.1 = bf16[6,128,128]{2,0,1:T(8,128)(2,1)S(1)} async-done(((bf16[6,128,128]{2,0,1:T(8,128)(2,1)}), bf16[6,128,128]{2,0,1:T(8,128)(2,1)S(1)}, u32[]{:S(2)}, u32[]{:S(2)}) %all-to-all-start.1) | async-done | bytes 196640 | tf_op jit(solution)/shard_map/all_to_all | solution.py:47
  30.8 6.5 %all-to-all-start = ((bf16[4,6,2,128,128]{4,2,1,0,3:T(2,128)(2,1)}), bf16[4,6,2,128,128]{4,2,1,0,3:T(2,128)(2,1)}, u32[]{:S(2)}, u32[]{:S(2)}) async-start(bf16[4,6,2,128,128]{4,2,1,0,3:T(2,128)(2,1)} %copy.29), calls=%async_computation | async-start | bytes 3145728 | tf_op jit(solution)/shard_map/all_to_all | solution.py:55
  37.3 0.0 all-gather.5.cloned.1.call-start
  37.4 0.1 fusion.23
  37.4 0.0 copy-done.5
  37.4 0.1 add_divide_fusion
  37.5 0.1 copy.33
  37.6 36.3 %all-to-all-done = bf16[4,6,2,128,128]{4,2,1,0,3:T(2,128)(2,1)} async-done(((bf16[4,6,2,128,128]{4,2,1,0,3:T(2,128)(2,1)}), bf16[4,6,2,128,128]{4,2,1,0,3:T(2,128)(2,1)}, u32[]{:S(2)}, u32[]{:S(2)}) %all-to-all-start) | async-done | bytes 1572896 | tf_op jit(solution)/shard_map/all_to_all | solution.py:55
  73.9 1.8 copy.30
  75.8 1.7 copy.31
  77.4 3.8 %fusion.5 = bf16[4,192,2,4,128]{4,1,2,0,3:T(8,128)(2,1)} fusion(bf16[4,192,2,4,128]{4,3,2,1,0:T(4,128)(2,1)} %bitcast.62, f32[128,128]{0,1:T(8,128)S(1)} %add_divide_fusion, f32[4,128]{1,0:T(4,128)S(1)} %fusion.23, bf16[192,4,128,1,1]{2,1,0,4,3:T(4,128)(2,1)S(1)} %bitcast.64), kind=kOutput, calls=%fused_computation.16 | convolution fusion | flops 405012480 | bytes 3409920 | tf_op jit(solution)/shard_map/lmn,brmnc->blrmc/dot_general | solution.py:60
  81.2 3.0 %copy.38 = bf16[4,192,2,4,128]{4,2,0,3,1:T(2,128)(2,1)S(1)} copy(bf16[4,192,2,4,128]{4,1,2,0,3:T(8,128)(2,1)} %fusion.5) | data formatting | bytes 3145728 | tf_op jit(solution)/shard_map/convert_element_type | solution.py:62
  84.3 43.7 %all_to_all.51 = bf16[4,192,2,4,128]{4,2,0,3,1:T(2,128)(2,1)S(1)} all-to-all(bf16[4,192,2,4,128]{4,2,0,3,1:T(2,128)(2,1)S(1)} %copy.38), channel_id=1, replica_groups=mesh['grp'=8,'lat'=32] {'lat'}, dimensions={1} | all-to-all | bytes 3145728 | tf_op jit(solution)/shard_map/all_to_all | solution.py:63
  128.0 0.8 copy.39
  128.8 0.9 copy.40
  129.7 0.8 fusion.21
  130.5 0.0 copy-start.1
  130.5 2.2 copy-done.1
  132.7 0.0 copy-start.4
  132.7 0.3 bitcast_convert_fusion
  132.9 0.6 copy-done.4
  133.5 0.0 copy-start.6
  133.5 0.0 copy-start.7
  133.5 0.0 copy-start.9
  133.5 5.0 %fusion.32 = f32[9216,256]{1,0:T(8,128)} fusion(bf16[9216,128]{1,0:T(8,128)(2,1)S(1)} %bitcast_convert_fusion, bf16[128,256]{1,0:T(8,128)(2,1)S(1)} %copy-done.4), kind=kOutput, calls=%fused_computation.48 | convolution fusion | flops 603979776 | bytes 11862016 | tf_op jit(solution)/shard_map/dot_general | solution.py:70
  138.5 0.0 copy-done
  138.5 0.0 copy-done.6
  138.5 0.0 copy-done.7
  138.5 0.0 copy-done.9
  138.5 0.0 copy-start.8
  138.6 7.6 %fusion.2 = f32[9216,256]{1,0:T(8,128)} fusion(bf16[256,256]{1,0:T(8,128)(2,1)S(1)} %copy-done.6, f32[9216,256]{1,0:T(8,128)} %fusion.32, bf16[9216,128]{1,0:T(8,128)(2,1)S(1)} %bitcast.51, bf16[128,256]{1,0:T(8,128)(2,1)S(1)} %copy-done.7, f32[256]{0:T(256)S(1)} %copy-done.9), kind=kOutput, calls=%fused_computation.10 | convolution fusion | flops 1828454400 | bytes 21431296 | tf_op jit(solution)/shard_map/dot_general | solution.py:78
  146.2 0.0 copy-done.8
  146.2 9.1 %fusion.1 = bf16[9216,128]{1,0:T(8,128)(2,1)} fusion(f32[9216,128]{1,0:T(8,128)} %bitcast.52, bf16[256,128]{1,0:T(8,128)(2,1)S(1)} %copy-done.8, f32[9216,256]{1,0:T(8,128)} %fusion.2), kind=kOutput, calls=%fused_computation.3 | convolution fusion | flops 618135552 | bytes 16580608 | tf_op jit(solution)/shard_map/dot_general | solution.py:80
  155.2 3.0 %reduce_sum.39 = bf16[6,384,128]{2,1,0:T(8,128)(2,1)} reduce(bf16[4,6,384,128]{3,2,1,0:T(8,128)(2,1)} %bitcast.53, bf16[]{:T(256)} %constant.37.clone.1), dimensions={0}, to_apply=%region_0.1 | reduce | flops 884736 | bytes 2949122 | tf_op jit(solution)/shard_map/reduce_sum | solution.py:84
  158.3 0.0 all-gather.5.cloned.1.call-update
  158.3 0.0 all-gather.7.cloned.1.call-start
  158.3 37.7 %all-gather.5.cloned.1.call-done = bf16[48,384,128]{2,1,0:T(8,128)(2,1)} async-done(((bf16[6,384,128]{2,1,0:T(8,128)(2,1)}), bf16[48,384,128]{2,1,0:T(8,128)(2,1)}) %all-gather.5.cloned.1.call-update) | async-done | bytes 4718608 | tf_op jit(solution)/shard_map/all_gather | solution.py:10
  196.0 3.2 %convert_reduce_fusion.1 = f32[6,384,128]{2,1,0:T(8,128)S(1)} fusion(bf16[8,6,384,128]{3,2,1,0:T(8,128)(2,1)} %bitcast.60), kind=kLoop, calls=%fused_computation.5 | loop fusion | flops 4423680 | bytes 5898240 | tf_op jit(solution)/shard_map/reduce_sum | solution.py:10
  199.2 0.0 copy-start.2
  199.2 0.1 broadcast_multiply_fusion.1
  199.3 1.6 copy-done.2
  200.9 0.0 copy-start.3
  200.9 1.5 multiply_reduce_fusion
  202.4 0.0 all-gather.7.cloned.1.call-update
  202.4 0.0 copy-done.3
  202.5 36.9 %all-gather.7.cloned.1.call-done = bf16[48,384,128]{2,1,0:T(8,128)(2,1)} async-done(((bf16[6,384,128]{2,1,0:T(8,128)(2,1)}), bf16[48,384,128]{2,1,0:T(8,128)(2,1)}) %all-gather.7.cloned.1.call-update) | async-done | bytes 4718608 | tf_op jit(solution)/shard_map/all_gather | solution.py:10
  239.4 3.2 %convert_reduce_fusion = f32[6,384,128]{2,1,0:T(8,128)S(1)} fusion(bf16[8,6,384,128]{3,2,1,0:T(8,128)(2,1)} %bitcast.61), kind=kLoop, calls=%fused_computation.4 | loop fusion | flops 4423680 | bytes 5898240 | tf_op jit(solution)/shard_map/reduce_sum | solution.py:10
  242.6 1.1 broadcast_multiply_fusion
  (2 shorter events, 0.0 us)
Async XLA Ops:
  7.2 131.4 %copy-start = (bf16[4,6,384,128]{3,2,1,0:T(8,128)(2,1)S(1)}, bf16[4,6,384,128]{3,2,1,0:T(8,128)(2,1)}, u32[]{:S(2)}) copy-start(bf16[4,6,384,128]{3,2,1,0:T(8,128)(2,1)} %param.10) | copy-start | bytes 7077892
  9.1 21.7 %all-to-all-start.1 = ((bf16[6,128,128]{2,0,1:T(8,128)(2,1)}), bf16[6,128,128]{2,0,1:T(8,128)(2,1)S(1)}, u32[]{:S(2)}, u32[]{:S(2)}) async-start(bf16[6,128,128]{2,0,1:T(8,128)(2,1)} %copy.32), calls=%async_computation.1 | async-start | bytes 524288 | tf_op jit(solution)/shard_map/all_to_all | solution.py:47
  27.4 10.1 %copy-start.5 = (f32[128]{0:T(128)S(1)}, f32[128]{0:T(128)}, u32[]{:S(2)}) copy-start(f32[128]{0:T(128)} %param.12) | copy-start | bytes 1540
  30.8 43.1 %all-to-all-start = ((bf16[4,6,2,128,128]{4,2,1,0,3:T(2,128)(2,1)}), bf16[4,6,2,128,128]{4,2,1,0,3:T(2,128)(2,1)}, u32[]{:S(2)}, u32[]{:S(2)}) async-start(bf16[4,6,2,128,128]{4,2,1,0,3:T(2,128)(2,1)} %copy.29), calls=%async_computation | async-start | bytes 3145728 | tf_op jit(solution)/shard_map/all_to_all | solution.py:55
  37.3 158.8 %all-gather.5.cloned.1.call-start = ((), (), s32[]{:S(2)}) async-start(), calls=%async_computation.3 | async-start | bytes 5308416 | tf_op jit(solution)/shard_map/all_gather | solution.py:10
  130.5 2.2 copy-start.1
  132.7 0.8 copy-start.4
  133.5 5.0 %copy-start.6 = (bf16[256,256]{1,0:T(8,128)(2,1)S(1)}, bf16[256,256]{1,0:T(8,128)(2,1)}, u32[]{:S(2)}) copy-start(bf16[256,256]{1,0:T(8,128)(2,1)} %param.16) | copy-start | bytes 393220
  133.5 5.0 %copy-start.7 = (bf16[128,256]{1,0:T(8,128)(2,1)S(1)}, bf16[128,256]{1,0:T(8,128)(2,1)}, u32[]{:S(2)}) copy-start(bf16[128,256]{1,0:T(8,128)(2,1)} %param.14) | copy-start | bytes 196612
  133.5 5.0 %copy-start.9 = (f32[256]{0:T(256)S(1)}, f32[256]{0:T(256)}, u32[]{:S(2)}) copy-start(f32[256]{0:T(256)} %param.15) | copy-start | bytes 3076
  138.5 7.6 %copy-start.8 = (bf16[256,128]{1,0:T(8,128)(2,1)S(1)}, bf16[256,128]{1,0:T(8,128)(2,1)}, u32[]{:S(2)}) copy-start(bf16[256,128]{1,0:T(8,128)(2,1)} %param.17) | copy-start | bytes 196612
  158.3 81.1 %all-gather.7.cloned.1.call-start = ((), (), s32[]{:S(2)}) async-start(), calls=%async_computation.4 | async-start | bytes 5308416 | tf_op jit(solution)/shard_map/all_gather | solution.py:10
  199.2 1.7 copy-start.2
  200.9 1.6 copy-start.3
Sparse Core Ops, SparseCore 0:
  158.4 37.5 all-gather.4
  202.6 36.7 all-gather.6
where the time goes:
time: 251 us
  waiting for transfers between devices  114 us (45%)
  blocking collectives  43.7 us (17%)
  matrix products  29 us (12%)
  starting transfers between devices  18.6 us (7%)
  local copies, waits for them, and re-layouts  17.3 us (7%)
  between operations  14.2 us (6%)
  other arithmetic  13.3 us (5%)
    all_gather x2, waiting for transfers between devices, total_of_pieces(): return lax.all_gather(x, axis).astype(jnp.float32).sum(0)  74.7 us
    all_to_all x1, blocking collectives, per_device(): lax.all_to_all(banded_grid, 'lat', split_axis=1, concat_axis=3, tiled=True)  43.7 us
    all_to_all x1, waiting for transfers between devices, per_device(): lax.all_to_all(fourier, 'lat', split_axis=3, concat_axis=1, tiled=True)  36.3 us
    all_to_all x1, starting transfers between devices, per_device(): lax.all_to_all(legendre, 'lat', split_axis=1, concat_axis=0, tiled=True)  12 us
    dot_general x1, matrix products, per_device(): jnp.dot(hidden_two, output_weight, preferred_element_type=jnp.float32)  9.08 us
    dot_general x1, matrix products, per_device(): jnp.dot(hidden_one, middle_weight, preferred_element_type=jnp.float32)  7.59 us
    all_to_all x1, starting transfers between devices, per_device(): lax.all_to_all(fourier, 'lat', split_axis=3, concat_axis=1, tiled=True)  6.47 us
    reduce_sum x2, other arithmetic, total_of_pieces(): return lax.all_gather(x, axis).astype(jnp.float32).sum(0)  6.35 us
  transfers between devices with their start and end apart: 4, of which 4 were waited for; matrix products, arithmetic and copies ran while one was open for 3% of the time, Pallas kernels for 0%

commit v1 on v0

v1 whole, which is shorter than its diff:
```python
import functools
import math

import jax
import jax.numpy as jnp
from jax import lax
from jax.experimental import pallas as pl
from jax.experimental.pallas import tpu as pltpu
from jax.sharding import PartitionSpec as P

MESH = pl.DeviceIdType.MESH
F32 = jnp.float32
BF16 = jnp.bfloat16

NY, NZ = 4, 8
NT = NY * NZ
NG = 8
NB = 4
NL = 6
LP = 3
NX = 384
C = 128
MX = NX // NG


def dot(a, b):
    return jnp.dot(a, b, preferred_element_type=F32)


def silu(v):
    u = 0.5 * v
    return u + u * jnp.tanh(u)


def kernel(
    grid_h, noise_h, leg_h, tf, ti, damp, wcat, bias, wmid, wout,
    new_h, mean_h, var_h,
    gbuf, nbuf, obuf, leg, lsend, lrecv, send1, recv1, send2, recv2,
    work_a, work_b, pn, pt, dm, msend, mrecv, asend, arecv, mbuf, vbuf,
    in_sem, out_sem, l_ss, l_rs, s1_ss, s1_rs, s2_ss, s2_rs, m_ss, m_rs, a_ss, a_rs,
):
    me = lax.axis_index("lat")
    mg = lax.axis_index("grp")
    my, mz = me // NZ, lax.rem(me, NZ)

    def peer(k):
        j, dy = k // NY, lax.rem(k, NY)
        half = (j + 1) // 2
        dz = jnp.where(lax.rem(j, 2) == 1, NZ - half, half)
        return lax.rem(my + dy, NY) * NZ + lax.rem(mz + dz, NZ)

    def each_peer(body):
        def step(k, carry):
            body(peer(NT - k))
            return carry
        lax.fori_loop(1, NT, step, 0)

    def each_mate(body):
        def step(k, carry):
            body(lax.rem(mg + k, NG))
            return carry
        lax.fori_loop(1, NG, step, 0)

    barrier = pltpu.get_barrier_semaphore()
    each_peer(lambda t: pl.semaphore_signal(
        barrier, inc=1, device_id={"lat": t}, device_id_type=MESH))
    each_mate(lambda g: pl.semaphore_signal(
        barrier, inc=1, device_id={"grp": g}, device_id_type=MESH))

    leg_in = pltpu.make_async_copy(leg_h, leg, in_sem.at[0])
    leg_in.start()
    g_in = [pltpu.make_async_copy(grid_h.at[b], gbuf.at[b], in_sem.at[1 + b]) for b in range(NB)]
    for c in g_in:
        c.start()
    n_in = pltpu.make_async_copy(noise_h, nbuf, in_sem.at[5])
    n_in.start()

    leg_in.wait()
    work_a[pl.ds(0, NL * C), :] = leg[...].astype(F32).reshape(NL * C, C)

    def pack_leg(p, carry):
        lsend[p] = work_a[pl.ds(p, 4 * NL, stride=NT), :].astype(BF16)
        return carry
    lax.fori_loop(0, NT, pack_leg, 0)

    def forward(b):
        for q in range(LP):
            rhs = jnp.concatenate([gbuf[b, 2 * q], gbuf[b, 2 * q + 1]], axis=1)
            out = dot(tf[...], rhs)
            both = jnp.concatenate(
                [out[:, :C].reshape(NT, 8, C), out[:, C:].reshape(NT, 8, C)], axis=1)
            send1[b, :, pl.ds(16 * q, 16), :] = both.astype(BF16)

    def send_first(b):
        each_peer(lambda t: pltpu.make_async_remote_copy(
            src_ref=send1.at[b, t], dst_ref=recv1.at[b, me],
            send_sem=s1_ss.at[b], recv_sem=s1_rs.at[b],
            device_id={"lat": t}, device_id_type=MESH).start())
        recv1[b, me] = send1[b, me]

    def all_bytes(ref, sem):
        pltpu.make_async_copy(ref, ref, sem).wait()

    g_in[0].wait()
    forward(0)
    pl.semaphore_wait(barrier, NT - 1 + NG - 1)
    each_peer(lambda t: pltpu.make_async_remote_copy(
        src_ref=lsend.at[t], dst_ref=lrecv.at[me],
        send_sem=l_ss, recv_sem=l_rs, device_id={"lat": t}, device_id_type=MESH).start())
    lrecv[me] = lsend[me]
    send_first(0)
    for b in range(1, NB):
        g_in[b].wait()
        forward(b)
        send_first(b)

    all_bytes(lrecv.at[pl.ds(0, NT - 1)], l_rs)
    work_a[pl.ds(0, NT * 4 * NL), :] = lrecv[...].astype(F32).reshape(NT * 4 * NL, C)
    rows = lax.broadcasted_iota(jnp.int32, (C, C), 0)
    for i in range(4):
        basis = work_a[pl.ds(i, NT * NL, stride=4), :]
        pn[i] = basis.astype(BF16)
        pt[i] = basis.T.astype(BF16)
        keep = rows >= me + NT * i
        dm[i] = jnp.where(keep, damp[...], 0.0)

    def legendre(b, carry):
        all_bytes(recv1.at[b, pl.ds(0, NT - 1)], s1_rs.at[b])
        work_a[...] = recv1[b].astype(F32).reshape(NT * 48, C)
        for i in range(4):
            x0 = work_a[pl.ds(i, NT * NL, stride=8), :].astype(BF16)
            x1 = work_a[pl.ds(4 + i, NT * NL, stride=8), :].astype(BF16)
            spec = dot(pt[i], jnp.concatenate([x0, x1], axis=1))
            scale = dm[i]
            filt = (spec * jnp.concatenate([scale, scale], axis=1)).astype(BF16)
            back = dot(pn[i], filt)
            work_b[pl.ds(i, NT * NL, stride=8), :] = back[:, :C]
            work_b[pl.ds(4 + i, NT * NL, stride=8), :] = back[:, C:]
        vals = work_b[...].astype(BF16).reshape(NT, LP, 16, C)
        for q in range(LP):
            send2[q, :, b] = vals[:, q]
        return carry
    lax.fori_loop(0, NB, legendre, 0)

    for q in range(LP):
        each_peer(lambda t: pltpu.make_async_remote_copy(
            src_ref=send2.at[q, t], dst_ref=recv2.at[q, me],
            send_sem=s2_ss.at[q], recv_sem=s2_rs.at[q],
            device_id={"lat": t}, device_id_type=MESH).start())
        recv2[q, me] = send2[q, me]

    def combine(q):
        all_bytes(mrecv.at[q, pl.ds(0, NG - 1)], m_rs.at[q])
        total = mrecv[q, 0, 0].astype(F32)
        square = mrecv[q, 0, 1].astype(F32)
        for g in range(1, NG):
            total += mrecv[q, g, 0].astype(F32)
            square += mrecv[q, g, 1].astype(F32)
        mean = total * (1.0 / (NB * NG))
        for g in range(NG):
            off = mrecv[q, g, 0].astype(F32) * (1.0 / NB) - mean
            square += NB * (off * off)
        asend[q, 0] = mean.astype(BF16)
        asend[q, 1] = (square * (1.0 / (NB * NG - 1))).astype(BF16)
        each_mate(lambda g: pltpu.make_async_remote_copy(
            src_ref=asend.at[q], dst_ref=arecv.at[q, mg],
            send_sem=a_ss.at[q], recv_sem=a_rs.at[q],
            device_id={"grp": g}, device_id_type=MESH).start())
        arecv[q, mg] = asend[q]

    def finish(q):
        all_bytes(arecv.at[q, pl.ds(0, NG - 1)], a_rs.at[q])
        for g in range(NG):
            mbuf[pl.ds(2 * q, 2), pl.ds(MX * g, MX), :] = arecv[q, g, 0].astype(F32)
            vbuf[pl.ds(2 * q, 2), pl.ds(MX * g, MX), :] = arecv[q, g, 1].astype(F32)
        pltpu.make_async_copy(mbuf.at[pl.ds(2 * q, 2)], mean_h.at[pl.ds(2 * q, 2)], out_sem.at[LP + q]).start()
        pltpu.make_async_copy(vbuf.at[pl.ds(2 * q, 2)], var_h.at[pl.ds(2 * q, 2)], out_sem.at[2 * LP + q]).start()

    n_in.wait()
    for q in range(LP):
        all_bytes(recv2.at[q, pl.ds(0, NT - 1)], s2_rs.at[q])

        def column(b, carry):
            vals = recv2[q, :, b].astype(F32)
            f0 = vals[:, :8].reshape(NT * 8, C).astype(BF16)
            f1 = vals[:, 8:].reshape(NT * 8, C).astype(BF16)
            smooth = dot(ti[...], jnp.concatenate([f0, f1], axis=1))
            smooth = jnp.concatenate([smooth[:, :C], smooth[:, C:]], axis=0)
            noise = nbuf[b, pl.ds(2 * q, 2)].reshape(2 * NX, C)
            pre = dot(jnp.concatenate([smooth.astype(BF16), noise], axis=1), wcat[...])
            one = silu(pre + bias[...]).astype(BF16)
            two = silu(dot(one, wmid[...])).astype(BF16)
            new = (smooth + dot(two, wout[...])).astype(BF16)
            obuf[b, pl.ds(2 * q, 2)] = new.reshape(2, NX, C)
            return carry
        lax.fori_loop(0, NB, column, 0)

        def moments(g, carry):
            vals = [obuf[b, pl.ds(2 * q, 2), pl.ds(MX * g, MX), :].astype(F32) for b in range(NB)]
            total = (vals[0] + vals[1]) + (vals[2] + vals[3])
            mean = total * (1.0 / NB)
            offs = [v - mean for v in vals]
            square = (offs[0] * offs[0] + offs[1] * offs[1]) + (offs[2] * offs[2] + offs[3] * offs[3])
            msend[q, g, 0] = total.astype(BF16)
            msend[q, g, 1] = square.astype(BF16)
            return carry
        lax.fori_loop(0, NG, moments, 0)
        each_mate(lambda g: pltpu.make_async_remote_copy(
            src_ref=msend.at[q, g], dst_ref=mrecv.at[q, mg],
            send_sem=m_ss.at[q], recv_sem=m_rs.at[q],
            device_id={"grp": g}, device_id_type=MESH).start())
        mrecv[q, mg] = msend[q, mg]
        pltpu.make_async_copy(
            obuf.at[:, pl.ds(2 * q, 2)], new_h.at[:, pl.ds(2 * q, 2)], out_sem.at[q]).start()
        if q >= 1:
            combine(q - 1)
        if q >= 2:
            finish(q - 2)
    combine(LP - 1)
    finish(LP - 2)
    finish(LP - 1)

    all_bytes(lsend.at[pl.ds(0, NT - 1)], l_ss)
    for b in range(NB):
        all_bytes(send1.at[b, pl.ds(0, NT - 1)], s1_ss.at[b])
    for q in range(LP):
        all_bytes(send2.at[q, pl.ds(0, NT - 1)], s2_ss.at[q])
        all_bytes(msend.at[q, pl.ds(0, NG - 1)], m_ss.at[q])
        all_bytes(mrecv.at[q, pl.ds(0, NG - 1)], a_ss.at[q])
        pltpu.make_async_copy(
            obuf.at[:, pl.ds(2 * q, 2)], new_h.at[:, pl.ds(2 * q, 2)], out_sem.at[q]).wait()
        pltpu.make_async_copy(mbuf.at[pl.ds(2 * q, 2)], mean_h.at[pl.ds(2 * q, 2)], out_sem.at[LP + q]).wait()
        pltpu.make_async_copy(vbuf.at[pl.ds(2 * q, 2)], var_h.at[pl.ds(2 * q, 2)], out_sem.at[2 * LP + q]).wait()


def wave_values(lon, order):
    peer_id, rest = order // 8, lax.rem(order, 8)
    part, wave = rest // 4, peer_id + NT * lax.rem(rest, 4)
    phase = lax.rem(lon * wave, NX).astype(F32) * (2.0 * math.pi / NX)
    value = jnp.where(part == 0, jnp.cos(phase), -jnp.sin(phase))
    return (value * math.sqrt(2.0 / NX)).astype(BF16)


def damping_filter(diffusion, wave_count):
    degree = jnp.arange(wave_count, dtype=jnp.int32).astype(F32)
    ratio = degree * (degree + 1.0) / float((wave_count - 1) * wave_count)
    return 1.0 / (1.0 + diffusion[None, :] * (ratio * ratio)[:, None])


def per_device(grid_state, noise_field, legendre, diffusion, input_weight, noise_weight, input_bias,
               middle_weight, output_weight):
    iota = functools.partial(lax.broadcasted_iota, jnp.int32)
    tf = wave_values(iota((2 * C, NX), 1), iota((2 * C, NX), 0))
    ti = wave_values(iota((NX, 2 * C), 0), iota((NX, 2 * C), 1))
    damp = damping_filter(diffusion, C)
    wcat = jnp.concatenate([input_weight, noise_weight], axis=0)
    vm = pl.BlockSpec(memory_space=pltpu.VMEM)
    hbm = pl.BlockSpec(memory_space=pl.ANY)
    dma = pltpu.SemaphoreType.DMA
    V = pltpu.VMEM
    return pl.pallas_call(
        kernel,
        out_shape=(
            jax.ShapeDtypeStruct((NB, NL, NX, C), BF16),
            jax.ShapeDtypeStruct((NL, NX, C), F32),
            jax.ShapeDtypeStruct((NL, NX, C), F32),
        ),
        in_specs=[hbm] * 3 + [vm] * 7,
        out_specs=(hbm, hbm, hbm),
        scratch_shapes=[
            V((NB, NL, NX, C), BF16), V((NB, NL, NX, C), BF16), V((NB, NL, NX, C), BF16),
            V((NL, C, C), BF16), V((NT, 4 * NL, C), BF16), V((NT, 4 * NL, C), BF16),
            V((NB, NT, 48, C), BF16), V((NB, NT, 48, C), BF16),
            V((LP, NT, NB, 16, C), BF16), V((LP, NT, NB, 16, C), BF16),
            V((NT * 48, C), F32), V((NT * 48, C), F32),
            V((4, NT * NL, C), BF16), V((4, C, NT * NL), BF16), V((4, C, C), F32),
            V((LP, NG, 2, 2, MX, C), BF16), V((LP, NG, 2, 2, MX, C), BF16),
            V((LP, 2, 2, MX, C), BF16), V((LP, NG, 2, 2, MX, C), BF16),
            V((NL, NX, C), F32), V((NL, NX, C), F32),
            dma((6,)), dma((3 * LP,)), dma, dma, dma((NB,)), dma((NB,)), dma((LP,)), dma((LP,)),
            dma((LP,)), dma((LP,)), dma((LP,)), dma((LP,)),
        ],
        compiler_params=pltpu.CompilerParams(
            collective_id=0, has_side_effects=True, vmem_limit_bytes=60 * 1024 * 1024),
    )(grid_state, noise_field, legendre, tf, ti, damp, wcat, input_bias[None, :], middle_weight, output_weight)


def solution(mesh):
    in_specs = (P("grp", "lat", None, None), P("grp", "lat", None, None), P("lat", None, None)) + (P(),) * 6
    out_specs = (P("grp", "lat", None, None), P("lat", None, None), P("lat", None, None))
    return jax.shard_map(per_device, mesh=mesh, in_specs=in_specs, out_specs=out_specs, check_vma=False)
```

time: 251 us -> 123 us (0.49)
  waiting for transfers between devices: 114 us -> 0 us
  Pallas kernels: 0 us -> 109 us
  blocking collectives: 43.7 us -> 0 us
  matrix products: 29 us -> 0 us
  starting transfers between devices: 18.6 us -> 0 us
  between operations: 14.2 us -> 0.69 us
  local copies, waits for them, and re-layouts: 17.3 us -> 5.48 us
  other arithmetic: 13.3 us -> 8.17 us
    pallas_call x0 -> x1, Pallas kernels: none -> 109 us  [per_device(): pl.pallas_call(kernel, out_shape=(jax.ShapeDtypeStruct((NB, NL, NX, C), B...]
    all_gather x2 -> x0, waiting for transfers between devices: 74.7 us -> none  [total_of_pieces(): return lax.all_gather(x, axis).astype(jnp.float32).sum(0)]
    all_to_all x1 -> x0, blocking collectives: 43.7 us -> none  [per_device(): lax.all_to_all(banded_grid, 'lat', split_axis=1, concat_axis=3, tiled=True)]
    all_to_all x2 -> x0, waiting for transfers between devices: 39.8 us -> none  [the longest x1 36.3 us: per_device(): lax.all_to_all(fourier, 'lat', split_axis=3, concat_axis=1, tiled=True)]
    dot_general x6 -> x0, matrix products: 29 us -> none  [the longest x1 9.08 us: per_device(): jnp.dot(hidden_two, output_weight, preferred_element_type=jnp.float32)]
    all_to_all x2 -> x0, starting transfers between devices: 18.5 us -> none  [the longest x1 12 us: per_device(): lax.all_to_all(legendre, 'lat', split_axis=1, concat_axis=0, tiled=True)]
    reduce_sum x4 -> x0, other arithmetic: 10.9 us -> none  [the longest x2 6.35 us: total_of_pieces(): return lax.all_gather(x, axis).astype(jnp.float32).sum(0)]
    all_to_all x5 -> x0, local copies, waits for them, and re-layouts: 5.23 us -> none  [the longest x2 3.5 us: per_device(): lax.all_to_all(fourier, 'lat', split_axis=3, concat_axis=1, tiled=True)]
  transfers between devices with their start and end apart: 4 -> 0, of which waited for: 4 -> 0; matrix products, arithmetic and copies ran while one was open for 3% -> 0% of each run, Pallas kernels for 0% -> 0%
where the time goes in v1:
time: 123 us
  Pallas kernels  109 us (89%)
  other arithmetic  8.17 us (7%)
  local copies, waits for them, and re-layouts  5.48 us (4%)
    pallas_call x1, Pallas kernels, per_device(): pl.pallas_call(kernel, out_shape=(jax.ShapeDtypeStruct((NB, NL, NX, C), B...  109 us
    unnamed x7, local copies, waits for them, and re-layouts  5.48 us
    convert_element_type x2, other arithmetic, wave_values(): return (value * math.sqrt(2.0 / NX)).astype(BF16)  5.23 us

profile of v1, /device:TPU:1, one launch (start us, length us, event | category | flops | bytes accessed | tf_op | source)
XLA Modules:
  0.0 123.1 jit_solution(11821360771015883087)
XLA Ops:
  0.7 1.4 %add_divide_fusion.damp = f32[128,128]{1,0:T(8,128)} fusion(f32[128]{0:T(128)S(1)} %fusion.7, f32[128]{0:T(128)} %param.12), kind=kLoop, calls=%fused_computation.5 | loop fusion | flops 49152 | bytes 66560 | tf_op jit(solution)/shard_map/div | solution.py:247
  2.1 1.5 %pad_maximum_fusion.wcat = bf16[256,256]{1,0:T(8,128)(2,1)} fusion(bf16[128,256]{1,0:T(8,128)(2,1)} %param.14, bf16[128,256]{1,0:T(8,128)(2,1)} %param.13), kind=kLoop, calls=%fused_computation.4 | loop fusion | flops 262144 | bytes 262144 | tf_op jit(solution)/shard_map/concatenate | solution.py:256
  3.6 2.9 %multiply_convert_fusion.1.tf = bf16[256,384]{1,0:T(8,128)(2,1)} fusion(s32[256]{0:T(256)S(1)} %get-tuple-element.7, s32[256]{0:T(256)S(1)} %get-tuple-element.3, s32[256]{0:T(256)S(1)} %get-tuple-element.8, s32[256]{0:T(256)S(1)} %get-tuple-element.4, s32[256]{0:T(256)S(1)} %broadcast_add_fusion.1, pred[256]{0:T(512)(128)(4,1)S(1)} %get-tuple-element.5, ...), kind=kLoop, calls=%fused_computation.2 | loop fusion | flops 1179648 | bytes 202240 | tf_op jit(solution)/shard_map/convert_element_type | solution.py:241
  6.5 2.4 %multiply_convert_fusion.ti = bf16[384,256]{1,0:T(8,128)(2,1)} fusion(s32[256]{0:T(256)S(1)} %get-tuple-element.7, s32[256]{0:T(256)S(1)} %get-tuple-element.3, s32[256]{0:T(256)S(1)} %get-tuple-element.8, s32[256]{0:T(256)S(1)} %get-tuple-element.4, s32[256]{0:T(256)S(1)} %broadcast_add_fusion.1, pred[256]{0:T(512)(128)(4,1)S(1)} %get-tuple-element.5, ...), kind=kLoop, calls=%fused_computation | loop fusion | flops 1179648 | bytes 202240 | tf_op jit(solution)/shard_map/convert_element_type | solution.py:241
  8.8 108.8 %shard_map.112 = (bf16[4,6,384,128]{3,2,1,0:T(8,128)(2,1)}, f32[6,384,128]{2,1,0:T(8,128)}, f32[6,384,128]{2,1,0:T(8,128)}) custom-call(bf16[4,6,384,128]{3,2,1,0:T(8,128)(2,1)} %grid_h.1, bf16[4,6,384,128]{3,2,1,0:T(8,128)(2,1)} %noise_h.1, bf16[6,128,128]{2,1,0:T(8,128)(2,1)} %leg_h.1, bf16[256,384]{1,0:T(8,128)(2,1)} %multiply_convert_fusion.1.tf, ...), custom_call_target="tpu_custom_call" | custom-call | tf_op jit(solution)/shard_map/pallas_call | solution.py:261
  117.6 0.0 copy-start.1
  117.6 0.0 copy-start
  117.7 3.4 %copy.15 = bf16[4,6,384,128]{3,2,1,0:T(8,128)(2,1)} copy(bf16[4,6,384,128]{3,2,1,0:T(8,128)(2,1)} %get-tuple-element.12) | data formatting | bytes 4718592
  121.1 0.0 copy-done.1
  121.1 1.0 copy.16
  122.1 0.0 copy-done
  122.1 1.0 copy.17
  (5 shorter events, 0.0 us)
Async XLA Ops:
  117.6 3.5 %copy-start.1 = (f32[6,384,128]{2,1,0:T(8,128)S(1)}, f32[6,384,128]{2,1,0:T(8,128)}, u32[]{:S(2)}) copy-start(f32[6,384,128]{2,1,0:T(8,128)} %get-tuple-element.13) | copy-start | bytes 3538948
  117.6 4.5 %copy-start = (f32[6,384,128]{2,1,0:T(8,128)S(1)}, f32[6,384,128]{2,1,0:T(8,128)}, u32[]{:S(2)}) copy-start(f32[6,384,128]{2,1,0:T(8,128)} %get-tuple-element.14) | copy-start | bytes 3538948

commit v2 on v1

v2 whole, which is shorter than its diff:
```python
import math

import jax
import jax.numpy as jnp
from jax import lax
from jax.experimental import pallas as pl
from jax.experimental.pallas import tpu as pltpu
from jax.sharding import PartitionSpec as P

MESH = pl.DeviceIdType.MESH
F32 = jnp.float32
BF16 = jnp.bfloat16

NY, NZ = 4, 8
NT = NY * NZ
NX4 = 4
NG = 8
NB = 4
NP = 2
NL = 6
NX = 384
C = 128
H = 256
MX = NX // NG
CHUNKS = ((0, 2), (2, 2), (4, 1), (5, 1))
NQ = len(CHUNKS)
MATES = ((2, 0), (2, 1), (1, 0), (3, 0), (1, 1), (3, 1), (0, 1))


def dot(a, b):
    return jnp.dot(a, b, preferred_element_type=F32)


def silu(v):
    u = 0.5 * v
    return u + u * jnp.tanh(u)


def angle(lon, wave):
    return lax.rem(lon * wave, NX).astype(F32) * (2.0 * math.pi / NX)


def all_bytes(ref, sem):
    pltpu.make_async_copy(ref, ref, sem).wait()


def kernel(
    grid_h, noise_h, leg_h, diff_h, win_h, wnoise_h, bias_h, wmid_h, wout_h,
    obuf, mbuf, vbuf,
    gbuf, nbuf, leg, diff, wcat, bias, wmid, wout, cosa, sina, tf, ti,
    lsend, lrecv, send1, recv1, send2, recv2, work_a, work_b, pn, pt, dm,
    msend, mrecv, asend, arecv,
    in_sem, l_ss, l_rs, k_ss, k_rs, s1_ss, s1_rs, s2_ss, s2_rs, m_ss, m_rs, a_ss, a_rs,
):
    lat, mg = lax.axis_index("lat"), lax.axis_index("grp")
    my, mz = lat // NZ, lax.rem(lat, NZ)
    me = mz * NY + my
    mx, mc = mg // 2, lax.rem(mg, 2)

    def each_peer(body):
        def step(n, carry):
            k = NT - n
            j, dy = k // NY, lax.rem(k, NY)
            half = (j + 1) // 2
            dz = jnp.where(lax.rem(j, 2) == 1, NZ - half, half)
            y, z = lax.rem(my + dy, NY), lax.rem(mz + dz, NZ)
            body(y * NZ + z, z * NY + y)
            return carry
        lax.fori_loop(1, NT, step, 0)

    def each_mate(body):
        for dx, dc in MATES:
            body(lax.rem(mx + dx, NX4) * 2 + lax.rem(mc + dc, 2))

    loads = [
        (grid_h.at[0], gbuf.at[0]), (grid_h.at[1], gbuf.at[1]), (grid_h.at[2], gbuf.at[2]), (grid_h.at[3], gbuf.at[3]),
        (leg_h, leg), (diff_h, diff), (win_h, wcat.at[pl.ds(0, C)]), (wnoise_h, wcat.at[pl.ds(C, C)]),
        (bias_h, bias), (wmid_h, wmid), (wout_h, wout), (noise_h, nbuf),
    ]
    loads = [pltpu.make_async_copy(s, d, in_sem.at[n]) for n, (s, d) in enumerate(loads)]
    loads[0].start()
    barrier = pltpu.get_barrier_semaphore()
    each_peer(lambda t, s: pl.semaphore_signal(
        barrier, inc=1, device_id={"lat": t}, device_id_type=MESH))
    each_mate(lambda g: pl.semaphore_signal(
        barrier, inc=1, device_id={"grp": g}, device_id_type=MESH))
    for c in loads[1:]:
        c.start()

    with jax.named_scope("tables"):
        iota = lambda shape, dim: lax.broadcasted_iota(jnp.int32, shape, dim)
        base = angle(iota((NT, NX), 1), iota((NT, NX), 0))
        cosa[...] = jnp.cos(base)
        sina[...] = jnp.sin(base)
        part = iota((8, NX), 0)
        step = angle(iota((8, NX), 1), NT * lax.rem(part, 4))
        scale = math.sqrt(2.0 / NX)
        cosb, sinb = scale * jnp.cos(step), scale * jnp.sin(step)
        real = part < 4
        u, v = jnp.where(real, cosb, -sinb), jnp.where(real, -sinb, -cosb)
        for j in range(NT // 2):
            pair = [cosa[pl.ds(p, 1), :] * u + sina[pl.ds(p, 1), :] * v for p in (2 * j, 2 * j + 1)]
            tf[pl.ds(16 * j, 16), :] = jnp.concatenate(pair, axis=0).astype(BF16)

    def forward(b):
        for q in range(NL // 2):
            rhs = jnp.concatenate([gbuf[b, 2 * q], gbuf[b, 2 * q + 1]], axis=1)
            out = dot(tf[...], rhs)
            both = jnp.concatenate(
                [out[:, :C].reshape(NT, 8, C), out[:, C:].reshape(NT, 8, C)], axis=1)
            send1[b, :, pl.ds(16 * q, 16), :] = both.astype(BF16)

    def send_first(b):
        each_peer(lambda t, s: pltpu.make_async_remote_copy(
            src_ref=send1.at[b, s], dst_ref=recv1.at[b, me],
            send_sem=s1_ss.at[b], recv_sem=s1_rs.at[b],
            device_id={"lat": t}, device_id_type=MESH).start())
        recv1[b, me] = send1[b, me]

    with jax.named_scope("w_g0"):
        loads[0].wait()
    with jax.named_scope("F0"):
        forward(0)
    loads[4].wait()

    source = mz == mg

    @pl.when(source)
    def _():
        work_a[pl.ds(0, NL * C), :] = leg[...].astype(F32).reshape(NL * C, C)

        def pack_leg(p, carry):
            lsend[p] = work_a[pl.ds(p, 4 * NL, stride=NT), :].astype(BF16)
            return carry
        lax.fori_loop(0, NT, pack_leg, 0)

    with jax.named_scope("barrier"):
        pl.semaphore_wait(barrier, NT - 1 + NG - 1)

    @pl.when(source)
    def _():
        each_peer(lambda t, s: pltpu.make_async_remote_copy(
            src_ref=lsend.at[s], dst_ref=lrecv.at[mz, my],
            send_sem=l_ss, recv_sem=l_rs, device_id={"lat": t}, device_id_type=MESH).start())
        lrecv[mz, my] = lsend[me]

    send_first(0)
    for b in range(1, NB):
        loads[b].wait()
        with jax.named_scope("F"):
            forward(b)
        with jax.named_scope("sF"):
            send_first(b)

    with jax.named_scope("w_leg"):
        @pl.when(source)
        def _():
            all_bytes(lrecv.at[mg, pl.ds(0, NY - 1)], l_rs)

        @pl.when(jnp.logical_not(source))
        def _():
            all_bytes(lrecv.at[mg], l_rs)

    each_mate(lambda g: pltpu.make_async_remote_copy(
        src_ref=lrecv.at[mg], dst_ref=lrecv.at[mg],
        send_sem=k_ss, recv_sem=k_rs, device_id={"grp": g}, device_id_type=MESH).start())
    with jax.named_scope("prep"):
        ti[...] = tf[...].astype(F32).T.astype(BF16)
        loads[5].wait()
        rows = iota((C, C), 0)
        degree = rows.astype(F32)
        ratio = degree * (degree + 1.0) / float((C - 1) * C)
        damp = 1.0 / (1.0 + diff[...] * (ratio * ratio))
        for i in range(4):
            dm[i] = jnp.where(rows >= me + NT * i, damp, 0.0)
    with jax.named_scope("w_k"):
        all_bytes(lrecv.at[pl.ds(0, NG - 1)], k_rs)
    with jax.named_scope("prepP"):
        work_a[pl.ds(0, NT * 4 * NL), :] = lrecv[...].astype(F32).reshape(NT * 4 * NL, C)
        for i in range(4):
            basis = work_a[pl.ds(i, NT * NL, stride=4), :]
            pn[i] = basis.astype(BF16)
            pt[i] = basis.T.astype(BF16)

    def send_second(l0, nl, pair, sem):
        def one(t, s):
            if pair is None:
                src, dst = send2.at[pl.ds(l0, nl), s], recv2.at[pl.ds(l0, nl), me]
            else:
                src, dst = send2.at[pl.ds(l0, nl), s, pair], recv2.at[pl.ds(l0, nl), me, pair]
            pltpu.make_async_remote_copy(
                src_ref=src, dst_ref=dst, send_sem=s2_ss.at[sem], recv_sem=s2_rs.at[sem],
                device_id={"lat": t}, device_id_type=MESH).start()
        each_peer(one)

    for pair in range(NP):
        def analyse(k, carry):
            b = NP * pair + k
            with jax.named_scope("w_a1"):
                all_bytes(recv1.at[b, pl.ds(0, NT - 1)], s1_rs.at[b])
            work_a[...] = recv1[b].astype(F32).reshape(NT * 48, C)
            for i in range(4):
                x0 = work_a[pl.ds(i, NT * NL, stride=8), :].astype(BF16)
                x1 = work_a[pl.ds(4 + i, NT * NL, stride=8), :].astype(BF16)
                spec = dot(pt[i], jnp.concatenate([x0, x1], axis=1))
                scale = dm[i]
                filt = (spec * jnp.concatenate([scale, scale], axis=1)).astype(BF16)
                back = dot(pn[i], filt)
                work_b[k, pl.ds(i, NT * NL, stride=8), :] = back[:, :C]
                work_b[k, pl.ds(4 + i, NT * NL, stride=8), :] = back[:, C:]
            return carry
        lax.fori_loop(0, 2, analyse, 0)
        vals = [work_b[k].reshape(NT, NL, 8, C) for k in range(2)]
        for l in range(NL):
            send2[l, :, pair] = jnp.concatenate([vals[0][:, l], vals[1][:, l]], axis=1).astype(BF16)
        with jax.named_scope("s2"):
            send_second(*CHUNKS[0], pair, pair)
    for q in range(1, NQ):
        send_second(*CHUNKS[q], None, q + 1)
    for l in range(NL):
        recv2[l, me] = send2[l, me]

    def combine(q):
        l0, nl = CHUNKS[q]
        with jax.named_scope("w_m"):
            all_bytes(mrecv.at[pl.ds(l0, nl), pl.ds(0, NG - 1)], m_rs.at[q])
        lats = pl.ds(l0, nl)
        total = mrecv[lats, 0, 0].astype(F32)
        square = mrecv[lats, 0, 1].astype(F32)
        for g in range(1, NG):
            total += mrecv[lats, g, 0].astype(F32)
            square += mrecv[lats, g, 1].astype(F32)
        mean = total * (1.0 / (NB * NG))
        for g in range(NG):
            off = mrecv[lats, g, 0].astype(F32) * (1.0 / NB) - mean
            square += NB * (off * off)
        asend[lats, 0] = mean.astype(BF16)
        asend[lats, 1] = (square * (1.0 / (NB * NG - 1))).astype(BF16)
        each_mate(lambda g: pltpu.make_async_remote_copy(
            src_ref=asend.at[lats], dst_ref=arecv.at[lats, mg],
            send_sem=a_ss.at[q], recv_sem=a_rs.at[q],
            device_id={"grp": g}, device_id_type=MESH).start())
        arecv[lats, mg] = asend[lats]

    def finish(q):
        l0, nl = CHUNKS[q]
        lats = pl.ds(l0, nl)
        with jax.named_scope("w_ag"):
            all_bytes(arecv.at[lats, pl.ds(0, NG - 1)], a_rs.at[q])
        for g in range(NG):
            mbuf[lats, pl.ds(MX * g, MX), :] = arecv[lats, g, 0].astype(F32)
            vbuf[lats, pl.ds(MX * g, MX), :] = arecv[lats, g, 1].astype(F32)

    for c in loads[6:]:
        c.wait()
    for q, (l0, nl) in enumerate(CHUNKS):
        with jax.named_scope("w_a2"):
            if q == 0:
                for pair in range(NP):
                    all_bytes(recv2.at[pl.ds(l0, nl), pl.ds(0, NT - 1), pair], s2_rs.at[pair])
            else:
                all_bytes(recv2.at[pl.ds(l0, nl), pl.ds(0, NT - 1)], s2_rs.at[q + 1])

        def column(n, carry):
            l, pair = l0 + n // NP, lax.rem(n, NP)
            vals = recv2[l, :, pair].astype(F32)
            f0 = vals[:, :8].reshape(NT * 8, C).astype(BF16)
            f1 = vals[:, 8:].reshape(NT * 8, C).astype(BF16)
            smooth = dot(ti[...], jnp.concatenate([f0, f1], axis=1))
            smooth = jnp.concatenate([smooth[:, :C], smooth[:, C:]], axis=0)
            noise = nbuf[pl.ds(2 * pair, 2), l].reshape(2 * NX, C)
            pre = dot(jnp.concatenate([smooth.astype(BF16), noise], axis=1), wcat[...])
            one = silu(pre + bias[...]).astype(BF16)
            two = silu(dot(one, wmid[...])).astype(BF16)
            new = (smooth + dot(two, wout[...])).astype(BF16)
            obuf[pl.ds(2 * pair, 2), l] = new.reshape(2, NX, C)
            return carry
        with jax.named_scope("G"):
            lax.fori_loop(0, nl * NP, column, 0)

        def moments(g, carry):
            lats = pl.ds(l0, nl)
            vals = [obuf[b, lats, pl.ds(MX * g, MX), :].astype(F32) for b in range(NB)]
            total = (vals[0] + vals[1]) + (vals[2] + vals[3])
            mean = total * (1.0 / NB)
            offs = [v - mean for v in vals]
            square = (offs[0] * offs[0] + offs[1] * offs[1]) + (offs[2] * offs[2] + offs[3] * offs[3])
            msend[lats, g, 0] = total.astype(BF16)
            msend[lats, g, 1] = square.astype(BF16)
            return carry
        with jax.named_scope("mom"):
            lax.fori_loop(0, NG, moments, 0)
        lats = pl.ds(l0, nl)
        each_mate(lambda g: pltpu.make_async_remote_copy(
            src_ref=msend.at[lats, g], dst_ref=mrecv.at[lats, mg],
            send_sem=m_ss.at[q], recv_sem=m_rs.at[q],
            device_id={"grp": g}, device_id_type=MESH).start())
        mrecv[lats, mg] = msend[lats, mg]
        if q >= 1:
            combine(q - 1)
        if q >= 2:
            finish(q - 2)
    combine(NQ - 1)
    finish(NQ - 2)
    finish(NQ - 1)

    with jax.named_scope("end"):
        @pl.when(source)
        def _():
            all_bytes(lsend.at[pl.ds(0, NT - 1)], l_ss)
        all_bytes(lrecv.at[pl.ds(0, NG - 1)], k_ss)
        for b in range(NB):
            all_bytes(send1.at[b, pl.ds(0, NT - 1)], s1_ss.at[b])
        for q, (l0, nl) in enumerate(CHUNKS):
            lats = pl.ds(l0, nl)
            if q == 0:
                for pair in range(NP):
                    all_bytes(send2.at[lats, pl.ds(0, NT - 1), pair], s2_ss.at[pair])
            else:
                all_bytes(send2.at[lats, pl.ds(0, NT - 1)], s2_ss.at[q + 1])
            all_bytes(msend.at[lats, pl.ds(0, NG - 1)], m_ss.at[q])
            all_bytes(arecv.at[lats, pl.ds(0, NG - 1)], a_ss.at[q])


def per_device(grid_state, noise_field, legendre, diffusion, input_weight, noise_weight, input_bias,
               middle_weight, output_weight):
    hbm = pl.BlockSpec(memory_space=pltpu.HBM)
    vm = pl.BlockSpec(memory_space=pltpu.VMEM)
    dma = pltpu.SemaphoreType.DMA
    V = pltpu.VMEM
    shapes = (((NB, NL, NX, C), BF16), ((NL, NX, C), F32), ((NL, NX, C), F32))
    return pl.pallas_call(
        kernel,
        out_shape=tuple(V(s, d) for s, d in shapes),
        in_specs=[hbm] * 9,
        out_specs=(vm, vm, vm),
        scratch_shapes=[
            V((NB, NL, NX, C), BF16), V((NB, NL, NX, C), BF16), V((NL, C, C), BF16), V((1, C), F32),
            V((H, H), BF16), V((1, H), F32), V((H, H), BF16), V((H, C), BF16),
            V((NT, NX), F32), V((NT, NX), F32), V((2 * C, NX), BF16), V((NX, 2 * C), BF16),
            V((NT, 4 * NL, C), BF16), V((NZ, NY, 4 * NL, C), BF16),
            V((NB, NT, 48, C), BF16), V((NB, NT, 48, C), BF16),
            V((NL, NT, NP, 16, C), BF16), V((NL, NT, NP, 16, C), BF16),
            V((NT * 48, C), F32), V((2, NT * 48, C), F32),
            V((4, NT * NL, C), BF16), V((4, C, NT * NL), BF16), V((4, C, C), F32),
            V((NL, NG, 2, MX, C), BF16), V((NL, NG, 2, MX, C), BF16),
            V((NL, 2, MX, C), BF16), V((NL, NG, 2, MX, C), BF16),
            dma((12,)), dma, dma, dma, dma, dma((NB,)), dma((NB,)), dma((NQ + 1,)), dma((NQ + 1,)),
            dma((NQ,)), dma((NQ,)), dma((NQ,)), dma((NQ,)),
        ],
        compiler_params=pltpu.CompilerParams(
            collective_id=0, has_side_effects=True, vmem_limit_bytes=48 * 1024 * 1024),
    )(*[pltpu.with_memory_space_constraint(a, pltpu.HBM) for a in (
        grid_state, noise_field, legendre, diffusion[None, :], input_weight, noise_weight, input_bias[None, :],
        middle_weight, output_weight)])

def solution(mesh):
    in_specs = (P("grp", "lat", None, None), P("grp", "lat", None, None), P("lat", None, None)) + (P(),) * 6
    out_specs = (P("grp", "lat", None, None), P("lat", None, None), P("lat", None, None))
    return jax.shard_map(per_device, mesh=mesh, in_specs=in_specs, out_specs=out_specs, check_vma=False)
```

time: 123 us -> 105 us (0.85)
  other arithmetic: 8.17 us -> 0 us
  Pallas kernels: 109 us -> 101 us
  local copies, waits for them, and re-layouts: 5.48 us -> 3.43 us
    pallas_call x1, Pallas kernels: 109 us -> 101 us  [per_device(): pl.pallas_call(kernel, out_shape=tuple((V(s, d) for s, d in shapes)), in_...]
    convert_element_type x2 -> x0, other arithmetic: 5.23 us -> none  [wave_values(): return (value * math.sqrt(2.0 / NX)).astype(BF16)]
    unnamed x7 -> x3, local copies, waits for them, and re-layouts: 5.48 us -> 3.43 us
    concatenate x1 -> x0, other arithmetic: 1.53 us -> none  [per_device(): wcat = jnp.concatenate([input_weight, noise_weight], axis=0)]
    div x2 -> x0, other arithmetic: 1.37 us -> none  [the longest x1 1.37 us: damping_filter(): return 1.0 / (1.0 + diffusion[None, :] * (ratio * ratio)[:, None])]
where the time goes in v2:
time: 105 us
  Pallas kernels  101 us (96%)
  local copies, waits for them, and re-layouts  3.43 us (3%)
    pallas_call x1, Pallas kernels, per_device(): pl.pallas_call(kernel, out_shape=tuple((V(s, d) for s, d in shapes)), in_...  101 us
    unnamed x3, local copies, waits for them, and re-layouts  3.43 us

profile of v2, /device:TPU:1, one launch (start us, length us, event | category | flops | bytes accessed | tf_op | source)
XLA Modules:
  0.0 104.8 jit_solution(16095194419847967429)
XLA Ops:
  0.6 100.8 %shard_map.112 = (bf16[4,6,384,128]{3,2,1,0:T(8,128)(2,1)S(1)}, f32[6,384,128]{2,1,0:T(8,128)S(1)}, f32[6,384,128]{2,1,0:T(8,128)S(1)}) custom-call(bf16[4,6,384,128]{3,2,1,0:T(8,128)(2,1)} %grid_h.1, bf16[4,6,384,128]{3,2,1,0:T(8,128)(2,1)} %noise_h.1, bf16[6,128,128]{2,1,0:T(8,128)(2,1)} %leg_h.1, f32[1,128]{1,0:T(1,128)} %bitcast.3, ...), custom_call_target="tpu_custom_call" | custom-call | tf_op jit(solution)/shard_map/pallas_call | solution.py:332
  101.4 1.4 %copy.15 = bf16[4,6,384,128]{3,2,1,0:T(8,128)(2,1)} copy(bf16[4,6,384,128]{3,2,1,0:T(8,128)(2,1)S(1)} %get-tuple-element.3) | data formatting | bytes 4718592
  102.8 1.0 copy.16
  103.8 1.0 copy.17

commit v3 on v2

--- a/solution.py
+++ b/solution.py
@@ -298,11 +298,9 @@
         mrecv[lats, mg] = msend[lats, mg]
         if q >= 1:
             combine(q - 1)
-        if q >= 2:
-            finish(q - 2)
     combine(NQ - 1)
-    finish(NQ - 2)
-    finish(NQ - 1)
+    for q in range(NQ):
+        finish(q)
 
     with jax.named_scope("end"):
         @pl.when(source)
@@ -322,6 +320,15 @@
             all_bytes(arecv.at[lats, pl.ds(0, NG - 1)], a_ss.at[q])
 
 
+def write_out(o, m, v, new_h, mean_h, var_h, sem):
+    copies = [pltpu.make_async_copy(s, d, sem.at[n])
+              for n, (s, d) in enumerate(((o, new_h), (m, mean_h), (v, var_h)))]
+    for c in copies:
+        c.start()
+    for c in copies:
+        c.wait()
+
+
 def per_device(grid_state, noise_field, legendre, diffusion, input_weight, noise_weight, input_bias,
                middle_weight, output_weight):
     hbm = pl.BlockSpec(memory_space=pltpu.HBM)
@@ -329,7 +336,7 @@
     dma = pltpu.SemaphoreType.DMA
     V = pltpu.VMEM
     shapes = (((NB, NL, NX, C), BF16), ((NL, NX, C), F32), ((NL, NX, C), F32))
-    return pl.pallas_call(
+    held = pl.pallas_call(
         kernel,
         out_shape=tuple(V(s, d) for s, d in shapes),
         in_specs=[hbm] * 9,
@@ -353,6 +360,14 @@
     )(*[pltpu.with_memory_space_constraint(a, pltpu.HBM) for a in (
         grid_state, noise_field, legendre, diffusion[None, :], input_weight, noise_weight, input_bias[None, :],
         middle_weight, output_weight)])
+    return pl.pallas_call(
+        write_out,
+        out_shape=tuple(jax.ShapeDtypeStruct(s, d) for s, d in shapes),
+        in_specs=[vm] * 3,
+        out_specs=(hbm,) * 3,
+        scratch_shapes=[dma((3,))],
+        compiler_params=pltpu.CompilerParams(vmem_limit_bytes=1024 * 1024),
+    )(*[pltpu.with_memory_space_constraint(a, pltpu.VMEM) for a in held])
 
 def solution(mesh):
     in_specs = (P("grp", "lat", None, None), P("grp", "lat", None, None), P("lat", None, None)) + (P(),) * 6

time: 105 us -> 104 us (level)
  local copies, waits for them, and re-layouts: 3.43 us -> 0 us
  Pallas kernels: 101 us -> 103 us
    unnamed x3 -> x0, local copies, waits for them, and re-layouts: 3.43 us -> none
    pallas_call x0 -> x1, Pallas kernels: none -> 2.21 us  [per_device(): pl.pallas_call(write_out, out_shape=tuple((jax.ShapeDtypeStruct(s, d) for...]
where the time goes in v3:
time: 104 us
  Pallas kernels  103 us (99%)
    pallas_call x1, Pallas kernels, per_device(): pl.pallas_call(kernel, out_shape=tuple((V(s, d) for s, d in shapes)), in_...  101 us
    pallas_call x1, Pallas kernels, per_device(): pl.pallas_call(write_out, out_shape=tuple((jax.ShapeDtypeStruct(s, d) for...  2.21 us

profile of v3, /device:TPU:1, one launch (start us, length us, event | category | flops | bytes accessed | tf_op | source)
XLA Modules:
  0.0 103.6 jit_solution(18119154626185414872)
XLA Ops:
  0.6 100.8 %shard_map.112 = (bf16[4,6,384,128]{3,2,1,0:T(8,128)(2,1)S(1)}, f32[6,384,128]{2,1,0:T(8,128)S(1)}, f32[6,384,128]{2,1,0:T(8,128)S(1)}) custom-call(bf16[4,6,384,128]{3,2,1,0:T(8,128)(2,1)} %grid_h.1, bf16[4,6,384,128]{3,2,1,0:T(8,128)(2,1)} %noise_h.1, bf16[6,128,128]{2,1,0:T(8,128)(2,1)} %leg_h.1, f32[1,128]{1,0:T(1,128)} %bitcast.3, ...), custom_call_target="tpu_custom_call" | custom-call | tf_op jit(solution)/shard_map/pallas_call | solution.py:339
  101.4 2.2 %shard_map.113 = (bf16[4,6,384,128]{3,2,1,0:T(8,128)(2,1)}, f32[6,384,128]{2,1,0:T(8,128)}, f32[6,384,128]{2,1,0:T(8,128)}) custom-call(bf16[4,6,384,128]{3,2,1,0:T(8,128)(2,1)S(1)} %get-tuple-element.6.o, f32[6,384,128]{2,1,0:T(8,128)S(1)} %get-tuple-element.7.m, f32[6,384,128]{2,1,0:T(8,128)S(1)} %get-tuple-element.8.v), custom_call_target="tpu_custom_call" | custom-call | tf_op jit(solution)/shard_map/pallas_call | solution.py:363

commit v4 on v3

--- a/solution.py
+++ b/solution.py
@@ -25,6 +25,7 @@
 CHUNKS = ((0, 2), (2, 2), (4, 1), (5, 1))
 NQ = len(CHUNKS)
 MATES = ((2, 0), (2, 1), (1, 0), (3, 0), (1, 1), (3, 1), (0, 1))
+LINE = (2, 1, 3)
 
 
 def dot(a, b):
@@ -49,8 +50,8 @@
     obuf, mbuf, vbuf,
     gbuf, nbuf, leg, diff, wcat, bias, wmid, wout, cosa, sina, tf, ti,
     lsend, lrecv, send1, recv1, send2, recv2, work_a, work_b, pn, pt, dm,
-    msend, mrecv, asend, arecv,
-    in_sem, l_ss, l_rs, k_ss, k_rs, s1_ss, s1_rs, s2_ss, s2_rs, m_ss, m_rs, a_ss, a_rs,
+    msend, hrecv, csend, mrecv, asend, arecv,
+    in_sem, l_ss, l_rs, k_ss, k_rs, s1_ss, s1_rs, s2_ss, s2_rs, h_ss, h_rs, m_ss, m_rs, a_ss, a_rs,
 ):
     lat, mg = lax.axis_index("lat"), lax.axis_index("grp")
     my, mz = lat // NZ, lax.rem(lat, NZ)
@@ -220,20 +221,42 @@
     for l in range(NL):
         recv2[l, me] = send2[l, me]
 
+    def join(q):
+        l0, nl = CHUNKS[q]
+        lats = pl.ds(l0, nl)
+        with jax.named_scope("w_h"):
+            all_bytes(hrecv.at[lats], h_rs.at[q])
+
+        def one(x, carry):
+            mine, theirs = msend[lats, mc, x, 0].astype(F32), hrecv[lats, x, 0].astype(F32)
+            off = mine - theirs
+            square = msend[lats, mc, x, 1].astype(F32) + hrecv[lats, x, 1].astype(F32)
+            csend[lats, x, 0] = (mine + theirs).astype(BF16)
+            csend[lats, x, 1] = (square + off * off * (1.0 / (2 * NB))).astype(BF16)
+            return carry
+        lax.fori_loop(0, NX4, one, 0)
+        for dx in LINE:
+            x = lax.rem(mx + dx, NX4)
+            pltpu.make_async_remote_copy(
+                src_ref=csend.at[lats, x], dst_ref=mrecv.at[lats, mx],
+                send_sem=m_ss.at[q], recv_sem=m_rs.at[q],
+                device_id={"grp": x * 2 + mc}, device_id_type=MESH).start()
+        mrecv[lats, mx] = csend[lats, mx]
+
     def combine(q):
         l0, nl = CHUNKS[q]
         with jax.named_scope("w_m"):
-            all_bytes(mrecv.at[pl.ds(l0, nl), pl.ds(0, NG - 1)], m_rs.at[q])
+            all_bytes(mrecv.at[pl.ds(l0, nl), pl.ds(0, NX4 - 1)], m_rs.at[q])
         lats = pl.ds(l0, nl)
         total = mrecv[lats, 0, 0].astype(F32)
         square = mrecv[lats, 0, 1].astype(F32)
-        for g in range(1, NG):
-            total += mrecv[lats, g, 0].astype(F32)
-            square += mrecv[lats, g, 1].astype(F32)
+        for x in range(1, NX4):
+            total += mrecv[lats, x, 0].astype(F32)
+            square += mrecv[lats, x, 1].astype(F32)
         mean = total * (1.0 / (NB * NG))
-        for g in range(NG):
-            off = mrecv[lats, g, 0].astype(F32) * (1.0 / NB) - mean
-            square += NB * (off * off)
+        for x in range(NX4):
+            off = mrecv[lats, x, 0].astype(F32) * (1.0 / (2 * NB)) - mean
+            square += (2 * NB) * (off * off)
         asend[lats, 0] = mean.astype(BF16)
         asend[lats, 1] = (square * (1.0 / (NB * NG - 1))).astype(BF16)
         each_mate(lambda g: pltpu.make_async_remote_copy(
@@ -285,17 +308,18 @@
             mean = total * (1.0 / NB)
             offs = [v - mean for v in vals]
             square = (offs[0] * offs[0] + offs[1] * offs[1]) + (offs[2] * offs[2] + offs[3] * offs[3])
-            msend[lats, g, 0] = total.astype(BF16)
-            msend[lats, g, 1] = square.astype(BF16)
+            x, c = g // 2, lax.rem(g, 2)
+            msend[lats, c, x, 0] = total.astype(BF16)
+            msend[lats, c, x, 1] = square.astype(BF16)
             return carry
         with jax.named_scope("mom"):
             lax.fori_loop(0, NG, moments, 0)
         lats = pl.ds(l0, nl)
-        each_mate(lambda g: pltpu.make_async_remote_copy(
-            src_ref=msend.at[lats, g], dst_ref=mrecv.at[lats, mg],
-            send_sem=m_ss.at[q], recv_sem=m_rs.at[q],
-            device_id={"grp": g}, device_id_type=MESH).start())
-        mrecv[lats, mg] = msend[lats, mg]
+        pltpu.make_async_remote_copy(
+            src_ref=msend.at[lats, 1 - mc], dst_ref=hrecv.at[lats],
+            send_sem=h_ss.at[q], recv_sem=h_rs.at[q],
+            device_id={"grp": mx * 2 + 1 - mc}, device_id_type=MESH).start()
+        join(q)
         if q >= 1:
             combine(q - 1)
     combine(NQ - 1)
@@ -316,7 +340,8 @@
                     all_bytes(send2.at[lats, pl.ds(0, NT - 1), pair], s2_ss.at[pair])
             else:
                 all_bytes(send2.at[lats, pl.ds(0, NT - 1)], s2_ss.at[q + 1])
-            all_bytes(msend.at[lats, pl.ds(0, NG - 1)], m_ss.at[q])
+            all_bytes(hrecv.at[lats], h_ss.at[q])
+            all_bytes(mrecv.at[lats, pl.ds(0, NX4 - 1)], m_ss.at[q])
             all_bytes(arecv.at[lats, pl.ds(0, NG - 1)], a_ss.at[q])
 
 
@@ -350,10 +375,11 @@
             V((NL, NT, NP, 16, C), BF16), V((NL, NT, NP, 16, C), BF16),
             V((NT * 48, C), F32), V((2, NT * 48, C), F32),
             V((4, NT * NL, C), BF16), V((4, C, NT * NL), BF16), V((4, C, C), F32),
-            V((NL, NG, 2, MX, C), BF16), V((NL, NG, 2, MX, C), BF16),
+            V((NL, 2, NX4, 2, MX, C), BF16), V((NL, NX4, 2, MX, C), BF16),
+            V((NL, NX4, 2, MX, C), BF16), V((NL, NX4, 2, MX, C), BF16),
             V((NL, 2, MX, C), BF16), V((NL, NG, 2, MX, C), BF16),
             dma((12,)), dma, dma, dma, dma, dma((NB,)), dma((NB,)), dma((NQ + 1,)), dma((NQ + 1,)),
-            dma((NQ,)), dma((NQ,)), dma((NQ,)), dma((NQ,)),
+            dma((NQ,)), dma((NQ,)), dma((NQ,)), dma((NQ,)), dma((NQ,)), dma((NQ,)),
         ],
         compiler_params=pltpu.CompilerParams(
             collective_id=0, has_side_effects=True, vmem_limit_bytes=48 * 1024 * 1024),

time: 104 us -> 101 us (0.971)
  Pallas kernels: 103 us -> 101 us
    pallas_call x1, Pallas kernels: 101 us -> 98.5 us  [per_device(): pl.pallas_call(kernel, out_shape=tuple((V(s, d) for s, d in shapes)), in_...]
where the time goes in v4:
time: 101 us
  Pallas kernels  101 us (100%)
    pallas_call x1, Pallas kernels, per_device(): pl.pallas_call(kernel, out_shape=tuple((V(s, d) for s, d in shapes)), in_...  98.5 us
    pallas_call x1, Pallas kernels, per_device(): pl.pallas_call(write_out, out_shape=tuple((jax.ShapeDtypeStruct(s, d) for...  2.21 us

profile of v4, /device:TPU:1, one launch (start us, length us, event | category | flops | bytes accessed | tf_op | source)
XLA Modules:
  0.0 101.4 jit_solution(3220207808523500885)
XLA Ops:
  0.6 98.5 %shard_map.112 = (bf16[4,6,384,128]{3,2,1,0:T(8,128)(2,1)S(1)}, f32[6,384,128]{2,1,0:T(8,128)S(1)}, f32[6,384,128]{2,1,0:T(8,128)S(1)}) custom-call(bf16[4,6,384,128]{3,2,1,0:T(8,128)(2,1)} %grid_h.1, bf16[4,6,384,128]{3,2,1,0:T(8,128)(2,1)} %noise_h.1, bf16[6,128,128]{2,1,0:T(8,128)(2,1)} %leg_h.1, f32[1,128]{1,0:T(1,128)} %bitcast.3, ...), custom_call_target="tpu_custom_call" | custom-call | tf_op jit(solution)/shard_map/pallas_call | solution.py:364
  99.2 2.2 %shard_map.113 = (bf16[4,6,384,128]{3,2,1,0:T(8,128)(2,1)}, f32[6,384,128]{2,1,0:T(8,128)}, f32[6,384,128]{2,1,0:T(8,128)}) custom-call(bf16[4,6,384,128]{3,2,1,0:T(8,128)(2,1)S(1)} %get-tuple-element.6.o, f32[6,384,128]{2,1,0:T(8,128)S(1)} %get-tuple-element.7.m, f32[6,384,128]{2,1,0:T(8,128)S(1)} %get-tuple-element.8.v), custom_call_target="tpu_custom_call" | custom-call | tf_op jit(solution)/shard_map/pallas_call | solution.py:389

commit v5 on v4

--- a/solution.py
+++ b/solution.py
@@ -1,3 +1,4 @@
+import functools
 import math
 
 import jax
@@ -26,6 +27,11 @@
 NQ = len(CHUNKS)
 MATES = ((2, 0), (2, 1), (1, 0), (3, 0), (1, 1), (3, 1), (0, 1))
 LINE = (2, 1, 3)
+J = 6
+NW = 8
+SIZES = (32, 32, 24, 24, 16, 16, 8, 8)
+OFFS = (0, 32, 64, 88, 112, 128, 144, 152)
+NR = 160
 
 
 def dot(a, b):
@@ -43,35 +49,71 @@
 
 def all_bytes(ref, sem):
     pltpu.make_async_copy(ref, ref, sem).wait()
+
+
+def band_column(col):
+    wave = jnp.zeros_like(col)
+    start = jnp.zeros_like(col)
+    for w in range(1, NW):
+        wave = wave + jnp.where(col >= OFFS[w], 1, 0)
+        start = start + jnp.where(col >= OFFS[w], OFFS[w] - OFFS[w - 1], 0)
+    return wave, col - start + 8 * (wave // 2)
 
 
 def kernel(
     grid_h, noise_h, leg_h, diff_h, win_h, wnoise_h, bias_h, wmid_h, wout_h,
     obuf, mbuf, vbuf,
     gbuf, nbuf, leg, diff, wcat, bias, wmid, wout, cosa, sina, tf, ti,
-    lsend, lrecv, send1, recv1, send2, recv2, work_a, work_b, pn, pt, dm,
+    lsend, lrecv, qsend, qrecv, send1, recv1, send2a, recv2a, send2b, recv2b,
+    t1send, t1recv, t3send, t3recv, dmat, dtm, scale3, rf, rp_send, rp_recv, rm_send, rm_recv, fall,
+    zf, work_a, work_b, work_c, pn, pt, dm,
     msend, hrecv, csend, mrecv, asend, arecv,
-    in_sem, l_ss, l_rs, k_ss, k_rs, s1_ss, s1_rs, s2_ss, s2_rs, h_ss, h_rs, m_ss, m_rs, a_ss, a_rs,
+    in_sem, l_ss, l_rs, k_ss, k_rs, q_ss, q_rs, t1_ss, t1_rs, t3_ss, t3_rs, rs_ss, rs_rs, ag_ss, ag_rs,
+    s1_ss, s1_rs, s2_ss, s2_rs, h_ss, h_rs, m_ss, m_rs, a_ss, a_rs,
 ):
     lat, mg = lax.axis_index("lat"), lax.axis_index("grp")
     my, mz = lat // NZ, lax.rem(lat, NZ)
     me = mz * NY + my
     mx, mc = mg // 2, lax.rem(mg, 2)
+    iota = lambda shape, dim: lax.broadcasted_iota(jnp.int32, shape, dim)
+
+    def visit(j, dy, body):
+        half = (j + 1) // 2
+        dz = jnp.where(lax.rem(j, 2) == 1, NZ - half, half)
+        y, z = lax.rem(my + dy, NY), lax.rem(mz + dz, NZ)
+        body(y * NZ + z, z * NY + y)
 
     def each_peer(body):
         def step(n, carry):
             k = NT - n
-            j, dy = k // NY, lax.rem(k, NY)
-            half = (j + 1) // 2
-            dz = jnp.where(lax.rem(j, 2) == 1, NZ - half, half)
-            y, z = lax.rem(my + dy, NY), lax.rem(mz + dz, NZ)
-            body(y * NZ + z, z * NY + y)
+            visit(k // NY, lax.rem(k, NY), body)
             return carry
         lax.fori_loop(1, NT, step, 0)
+
+    def each_row(dy, body):
+        def step(n, carry):
+            visit(NZ - 1 - n, dy, body)
+            return carry
+        lax.fori_loop(0, NZ - (1 if dy == 0 else 0), step, 0)
 
     def each_mate(body):
         for dx, dc in MATES:
             body(lax.rem(mx + dx, NX4) * 2 + lax.rem(mc + dc, 2))
+
+    def each_y(body):
+        for dy in (2, 1, 3):
+            y = lax.rem(my + dy, NY)
+            body(y, y * NZ + mz)
+
+    def around(d):
+        return lax.rem(mz + d + NZ, NZ)
+
+    def send(src, dst, ss, rs, lat_id):
+        pltpu.make_async_remote_copy(
+            src_ref=src, dst_ref=dst, send_sem=ss, recv_sem=rs,
+            device_id={"lat": lat_id}, device_id_type=MESH).start()
+
+    up, down = my * NZ + around(1), my * NZ + around(-1)
 
     loads = [
         (grid_h.at[0], gbuf.at[0]), (grid_h.at[1], gbuf.at[1]), (grid_h.at[2], gbuf.at[2]), (grid_h.at[3], gbuf.at[3]),
@@ -80,16 +122,16 @@
     ]
     loads = [pltpu.make_async_copy(s, d, in_sem.at[n]) for n, (s, d) in enumerate(loads)]
     loads[0].start()
+    loads[1].start()
     barrier = pltpu.get_barrier_semaphore()
     each_peer(lambda t, s: pl.semaphore_signal(
         barrier, inc=1, device_id={"lat": t}, device_id_type=MESH))
     each_mate(lambda g: pl.semaphore_signal(
         barrier, inc=1, device_id={"grp": g}, device_id_type=MESH))
-    for c in loads[1:]:
+    for c in loads[2:]:
         c.start()
 
     with jax.named_scope("tables"):
-        iota = lambda shape, dim: lax.broadcasted_iota(jnp.int32, shape, dim)
         base = angle(iota((NT, NX), 1), iota((NT, NX), 0))
         cosa[...] = jnp.cos(base)
         sina[...] = jnp.sin(base)
@@ -99,60 +141,143 @@
         cosb, sinb = scale * jnp.cos(step), scale * jnp.sin(step)
         real = part < 4
         u, v = jnp.where(real, cosb, -sinb), jnp.where(real, -sinb, -cosb)
-        for j in range(NT // 2):
-            pair = [cosa[pl.ds(p, 1), :] * u + sina[pl.ds(p, 1), :] * v for p in (2 * j, 2 * j + 1)]
-            tf[pl.ds(16 * j, 16), :] = jnp.concatenate(pair, axis=0).astype(BF16)
+        for j in range(J):
+            k = 4 * (j // 3) + j % 3
+            tf[pl.ds(NT * j, NT), :] = (cosa[...] * u[k:k + 1] + sina[...] * v[k:k + 1]).astype(BF16)
+        row = iota((NT, NX), 0)
+        high = angle(iota((NT, NX), 1), NY * lax.rem(row, NW) + row // NW)
+        cosq, sinq = jnp.cos(high), jnp.sin(high)
+        for q in range(NY):
+            co, si = cosq[NW * q:NW * (q + 1)], sinq[NW * q:NW * (q + 1)]
+            pair = [co * u[k:k + 1] + si * v[k:k + 1] for k in (3, 7)]
+            tf[pl.ds(J * NT + 16 * q, 16), :] = jnp.concatenate(pair, axis=0).astype(BF16)
 
     def forward(b):
-        for q in range(NL // 2):
-            rhs = jnp.concatenate([gbuf[b, 2 * q], gbuf[b, 2 * q + 1]], axis=1)
+        loads[b].wait()
+        for n in range(NL // 2):
+            rhs = jnp.concatenate([gbuf[b, 2 * n], gbuf[b, 2 * n + 1]], axis=1)
             out = dot(tf[...], rhs)
-            both = jnp.concatenate(
-                [out[:, :C].reshape(NT, 8, C), out[:, C:].reshape(NT, 8, C)], axis=1)
-            send1[b, :, pl.ds(16 * q, 16), :] = both.astype(BF16)
-
-    def send_first(b):
-        each_peer(lambda t, s: pltpu.make_async_remote_copy(
-            src_ref=send1.at[b, s], dst_ref=recv1.at[b, me],
-            send_sem=s1_ss.at[b], recv_sem=s1_rs.at[b],
-            device_id={"lat": t}, device_id_type=MESH).start())
-        recv1[b, me] = send1[b, me]
-
-    with jax.named_scope("w_g0"):
-        loads[0].wait()
-    with jax.named_scope("F0"):
+            high = []
+            for k in range(2):
+                lanes = out[:, k * C:(k + 1) * C]
+                for j in range(J):
+                    zf[pl.ds((2 * n + k) * 2 * J + (b % 2) * J + j, NT, stride=NL * 2 * J), :] = (
+                        lanes[NT * j:NT * (j + 1)])
+                high.append(lanes[J * NT:].reshape(NY, 2, NW, C))
+            high = jnp.concatenate(high, axis=2).astype(BF16)
+            for r in range(2):
+                t1send[:, r * NB + b, pl.ds(16 * n, 16), :] = high[:, r]
+
+    def pack(pair):
+        send1[pair] = zf[...].astype(BF16).reshape(NT, NL * 2 * J, C)
+        recv1[pair, me] = send1[pair, me]
+
+    def send_first(pair, dy):
+        each_row(dy, lambda t, s: send(
+            send1.at[pair, s], recv1.at[pair, me], s1_ss.at[pair], s1_rs.at[pair], t))
+
+    with jax.named_scope("F01"):
         forward(0)
+        forward(1)
+        pack(0)
     loads[4].wait()
-
     source = mz == mg
+    with jax.named_scope("basis"):
+        work_a[pl.ds(0, NL * C), :] = leg[...].astype(F32).reshape(NL * C, C)
+        for q in range(NY):
+            band = [work_a[pl.ds(C * l + 3 * NT + q, NW, stride=NY), :] for l in range(NL)]
+            qsend[q] = jnp.concatenate(band, axis=0).astype(BF16)
+
+        @pl.when(source)
+        def _():
+            def pack_leg(p, carry):
+                lsend[p] = work_a[pl.ds(p, 4 * NL, stride=NT), :].astype(BF16)
+                return carry
+            lax.fori_loop(0, NT, pack_leg, 0)
+
+    with jax.named_scope("barrier"):
+        pl.semaphore_wait(barrier, NT - 1 + NG - 1)
 
     @pl.when(source)
     def _():
-        work_a[pl.ds(0, NL * C), :] = leg[...].astype(F32).reshape(NL * C, C)
-
-        def pack_leg(p, carry):
-            lsend[p] = work_a[pl.ds(p, 4 * NL, stride=NT), :].astype(BF16)
-            return carry
-        lax.fori_loop(0, NT, pack_leg, 0)
-
-    with jax.named_scope("barrier"):
-        pl.semaphore_wait(barrier, NT - 1 + NG - 1)
-
-    @pl.when(source)
-    def _():
-        each_peer(lambda t, s: pltpu.make_async_remote_copy(
-            src_ref=lsend.at[s], dst_ref=lrecv.at[mz, my],
-            send_sem=l_ss, recv_sem=l_rs, device_id={"lat": t}, device_id_type=MESH).start())
+        each_peer(lambda t, s: send(lsend.at[s], lrecv.at[mz, my], l_ss, l_rs, t))
         lrecv[mz, my] = lsend[me]
-
-    send_first(0)
-    for b in range(1, NB):
-        loads[b].wait()
-        with jax.named_scope("F"):
-            forward(b)
-        with jax.named_scope("sF"):
-            send_first(b)
-
+    send_first(0, 1)
+    each_y(lambda y, t: send(qsend.at[y], qrecv.at[my], q_ss, q_rs, t))
+    qrecv[my] = qsend[my]
+    send_first(0, 2)
+    with jax.named_scope("F23"):
+        forward(2)
+        forward(3)
+    each_y(lambda y, t: send(t1send.at[y], t1recv.at[my], t1_ss, t1_rs, t))
+    t1recv[my] = t1send[my]
+    with jax.named_scope("prep"):
+        pack(1)
+        loads[5].wait()
+        rows = iota((C, C), 0)
+
+        def damp_at(degree):
+            ratio = degree.astype(F32) * (degree.astype(F32) + 1.0) / float((C - 1) * C)
+            return 1.0 / (1.0 + diff[...] * (ratio * ratio))
+        damp = damp_at(rows)
+        for i in range(3):
+            dm[i] = jnp.where(rows >= me + NT * i, damp, 0.0)
+        wave, degree = band_column(iota((NR, C), 0))
+        scale3[...] = jnp.where(degree >= NY * wave + my, damp_at(degree + 3 * NT), 0.0)
+    with jax.named_scope("w_q"):
+        all_bytes(qrecv.at[pl.ds(0, NY - 1)], q_rs)
+    with jax.named_scope("dmat"):
+        col = iota((C, 2 * C), 1)
+        _, degree = band_column(col)
+        pick = jnp.where((col < NR) & (iota((C, 2 * C), 0) == degree + 3 * NT), 1.0, 0.0).astype(BF16)
+        spread = dot(qrecv[...].reshape(NY * NL * NW, C), pick)
+        wave, _ = band_column(iota((NY * NL * NW, 2 * C), 1))
+        spread = jnp.where(lax.rem(iota((NY * NL * NW, 2 * C), 0), NW) == wave, spread, 0.0)
+        dtm[...] = spread[:, :NR].astype(BF16)
+        dmat[...] = spread.T[:NR].astype(BF16)
+    with jax.named_scope("w_t1"):
+        all_bytes(t1recv.at[pl.ds(0, NY - 1)], t1_rs)
+    with jax.named_scope("R"):
+        for k in range(0, 8, 2):
+            both = [t1recv[:, k + e].reshape(NY * NL * NW, C) for e in range(2)]
+            out = dot(dmat[...], jnp.concatenate(both, axis=1))
+            rf[k] = out[:, :C]
+            rf[k + 1] = out[:, C:]
+
+    def reduce_send(k):
+        part = rf[around(4 - k)]
+        if k > 0:
+            part += rp_recv[k - 1].astype(F32)
+        rp_send[k] = part.astype(BF16)
+        if k < 3:
+            part = rf[around(k - 3)]
+            if k > 0:
+                part += rm_recv[k - 1].astype(F32)
+            rm_send[k] = part.astype(BF16)
+        send(rp_send.at[k], rp_recv.at[k], rs_ss.at[0, k], rs_rs.at[0, k], up)
+        if k < 3:
+            send(rm_send.at[k], rm_recv.at[k], rs_ss.at[1, k], rs_rs.at[1, k], down)
+
+    def reduce_wait(k):
+        with jax.named_scope("w_rs"):
+            all_bytes(rp_recv.at[k], rs_rs.at[0, k])
+            if k < 3:
+                all_bytes(rm_recv.at[k], rs_rs.at[1, k])
+
+    def gather_send(k):
+        a, b = around(-k), around(k)
+        send(fall.at[a], fall.at[a], ag_ss.at[0, k], ag_rs.at[0, k], up)
+        if k < 3:
+            send(fall.at[b], fall.at[b], ag_ss.at[1, k], ag_rs.at[1, k], down)
+
+    def gather_wait(k):
+        with jax.named_scope("w_ring"):
+            all_bytes(fall.at[0], ag_rs.at[0, k])
+            if k < 3:
+                all_bytes(fall.at[0], ag_rs.at[1, k])
+
+    reduce_send(0)
+    send_first(0, 3)
     with jax.named_scope("w_leg"):
         @pl.when(source)
         def _():
@@ -161,65 +286,91 @@
         @pl.when(jnp.logical_not(source))
         def _():
             all_bytes(lrecv.at[mg], l_rs)
-
     each_mate(lambda g: pltpu.make_async_remote_copy(
         src_ref=lrecv.at[mg], dst_ref=lrecv.at[mg],
         send_sem=k_ss, recv_sem=k_rs, device_id={"grp": g}, device_id_type=MESH).start())
-    with jax.named_scope("prep"):
+    reduce_wait(0)
+    reduce_send(1)
+    send_first(0, 0)
+    with jax.named_scope("prep2"):
         ti[...] = tf[...].astype(F32).T.astype(BF16)
-        loads[5].wait()
-        rows = iota((C, C), 0)
-        degree = rows.astype(F32)
-        ratio = degree * (degree + 1.0) / float((C - 1) * C)
-        damp = 1.0 / (1.0 + diff[...] * (ratio * ratio))
-        for i in range(4):
-            dm[i] = jnp.where(rows >= me + NT * i, damp, 0.0)
+    reduce_wait(1)
+    reduce_send(2)
+    send_first(1, 1)
     with jax.named_scope("w_k"):
         all_bytes(lrecv.at[pl.ds(0, NG - 1)], k_rs)
     with jax.named_scope("prepP"):
         work_a[pl.ds(0, NT * 4 * NL), :] = lrecv[...].astype(F32).reshape(NT * 4 * NL, C)
-        for i in range(4):
-            basis = work_a[pl.ds(i, NT * NL, stride=4), :]
+        for i in range(3):
+            basis = jnp.concatenate(
+                [work_a[pl.ds(4 * l + i, NT, stride=4 * NL), :] for l in range(NL)], axis=0)
             pn[i] = basis.astype(BF16)
             pt[i] = basis.T.astype(BF16)
-
-    def send_second(l0, nl, pair, sem):
-        def one(t, s):
-            if pair is None:
-                src, dst = send2.at[pl.ds(l0, nl), s], recv2.at[pl.ds(l0, nl), me]
-            else:
-                src, dst = send2.at[pl.ds(l0, nl), s, pair], recv2.at[pl.ds(l0, nl), me, pair]
-            pltpu.make_async_remote_copy(
-                src_ref=src, dst_ref=dst, send_sem=s2_ss.at[sem], recv_sem=s2_rs.at[sem],
-                device_id={"lat": t}, device_id_type=MESH).start()
-        each_peer(one)
-
-    for pair in range(NP):
-        def analyse(k, carry):
-            b = NP * pair + k
-            with jax.named_scope("w_a1"):
-                all_bytes(recv1.at[b, pl.ds(0, NT - 1)], s1_rs.at[b])
-            work_a[...] = recv1[b].astype(F32).reshape(NT * 48, C)
-            for i in range(4):
-                x0 = work_a[pl.ds(i, NT * NL, stride=8), :].astype(BF16)
-                x1 = work_a[pl.ds(4 + i, NT * NL, stride=8), :].astype(BF16)
-                spec = dot(pt[i], jnp.concatenate([x0, x1], axis=1))
+    reduce_wait(2)
+    reduce_send(3)
+    send_first(1, 2)
+    reduce_wait(3)
+    total = rf[mz] + rp_recv[3].astype(F32) + rm_recv[2].astype(F32)
+    fall[mz] = (total * scale3[...]).astype(BF16)
+    gather_send(0)
+    send_first(1, 3)
+    gather_wait(0)
+    gather_send(1)
+    send_first(1, 0)
+
+    def analyse(pair):
+        with jax.named_scope("w_a1"):
+            all_bytes(recv1.at[pair, pl.ds(0, NT - 1)], s1_rs.at[pair])
+
+        def member(k, carry):
+            for i in range(3):
+                halves = [jnp.concatenate(
+                    [work_a[pl.ds(2 * J * l + J * k + 3 * r + i, NT, stride=NL * 2 * J), :] for l in range(NL)],
+                    axis=0).astype(BF16) for r in range(2)]
+                spec = dot(pt[i], jnp.concatenate(halves, axis=1))
                 scale = dm[i]
                 filt = (spec * jnp.concatenate([scale, scale], axis=1)).astype(BF16)
                 back = dot(pn[i], filt)
-                work_b[k, pl.ds(i, NT * NL, stride=8), :] = back[:, :C]
-                work_b[k, pl.ds(4 + i, NT * NL, stride=8), :] = back[:, C:]
+                for r in range(2):
+                    j = 3 * r + i
+                    for l in range(NL):
+                        rows = back[NT * l:NT * (l + 1), r * C:(r + 1) * C]
+                        if l < 2:
+                            work_c[pl.ds(2 * J * l + J * k + j, NT, stride=4 * J), :] = rows
+                        else:
+                            work_b[l - 2, pl.ds(2 * J * pair + J * k + j, NT, stride=4 * J), :] = rows
             return carry
-        lax.fori_loop(0, 2, analyse, 0)
-        vals = [work_b[k].reshape(NT, NL, 8, C) for k in range(2)]
-        for l in range(NL):
-            send2[l, :, pair] = jnp.concatenate([vals[0][:, l], vals[1][:, l]], axis=1).astype(BF16)
-        with jax.named_scope("s2"):
-            send_second(*CHUNKS[0], pair, pair)
+        with jax.named_scope("S"):
+            work_a[...] = recv1[pair].astype(F32).reshape(NT * NL * 2 * J, C)
+            lax.fori_loop(0, 2, member, 0)
+            send2a[pair] = work_c[...].astype(BF16).reshape(NT, 4 * J, C)
+            if pair == 1:
+                for l in range(NL - 2):
+                    send2b[l] = work_b[l].astype(BF16).reshape(NT, 4 * J, C)
+        each_peer(lambda t, s: send(send2a.at[pair, s], recv2a.at[pair, me], s2_ss.at[pair], s2_rs.at[pair], t))
+        recv2a[pair, me] = send2a[pair, me]
+
+    gather_wait(1)
+    gather_send(2)
+    analyse(0)
+    gather_wait(2)
+    gather_send(3)
+    analyse(1)
     for q in range(1, NQ):
-        send_second(*CHUNKS[q], None, q + 1)
-    for l in range(NL):
-        recv2[l, me] = send2[l, me]
+        l0, nl = CHUNKS[q]
+        lats = pl.ds(l0 - 2, nl)
+        each_peer(lambda t, s: send(
+            send2b.at[lats, s], recv2b.at[lats, me], s2_ss.at[q + 1], s2_rs.at[q + 1], t))
+    for l in range(NL - 2):
+        recv2b[l, me] = send2b[l, me]
+    gather_wait(3)
+    with jax.named_scope("synth"):
+        for k in range(0, 8, 2):
+            out = dot(dtm[...], jnp.concatenate([fall[k], fall[k + 1]], axis=1)).astype(BF16)
+            t3send[:, k] = out[:, :C].reshape(NY, NL * NW, C)
+            t3send[:, k + 1] = out[:, C:].reshape(NY, NL * NW, C)
+    each_y(lambda y, t: send(t3send.at[y], t3recv.at[my], t3_ss, t3_rs, t))
+    t3recv[my] = t3send[my]
 
     def join(q):
         l0, nl = CHUNKS[q]
@@ -276,20 +427,32 @@
 
     for c in loads[6:]:
         c.wait()
+    with jax.named_scope("w_t3"):
+        all_bytes(t3recv.at[pl.ds(0, NY - 1)], t3_rs)
     for q, (l0, nl) in enumerate(CHUNKS):
         with jax.named_scope("w_a2"):
             if q == 0:
-                for pair in range(NP):
-                    all_bytes(recv2.at[pl.ds(l0, nl), pl.ds(0, NT - 1), pair], s2_rs.at[pair])
+                for pair in range(2):
+                    all_bytes(recv2a.at[pair, pl.ds(0, NT - 1)], s2_rs.at[pair])
             else:
-                all_bytes(recv2.at[pl.ds(l0, nl), pl.ds(0, NT - 1)], s2_rs.at[q + 1])
-
-        def column(n, carry):
-            l, pair = l0 + n // NP, lax.rem(n, NP)
-            vals = recv2[l, :, pair].astype(F32)
-            f0 = vals[:, :8].reshape(NT * 8, C).astype(BF16)
-            f1 = vals[:, 8:].reshape(NT * 8, C).astype(BF16)
-            smooth = dot(ti[...], jnp.concatenate([f0, f1], axis=1))
+                all_bytes(recv2b.at[pl.ds(l0 - 2, nl), pl.ds(0, NT - 1)], s2_rs.at[q + 1])
+
+        def column(l, pair, carry):
+            if l < 2:
+                work_c[...] = recv2a[pair].astype(F32).reshape(NT * 4 * J, C)
+                first = 2 * J * l
+            else:
+                work_c[...] = recv2b[l - 2].astype(F32).reshape(NT * 4 * J, C)
+                first = 2 * J * pair
+            sides = []
+            for k in range(2):
+                rows = [work_c[pl.ds(first + J * k + j, NT, stride=4 * J), :] for j in range(J)]
+                for y in range(NY):
+                    for r in range(2):
+                        two = t3recv[y, r * NB + 2 * pair + k, pl.ds(16 * (l // 2), 16), :].astype(F32)
+                        rows.append(two[8 * (l % 2):8 * (l % 2) + 8])
+                sides.append(jnp.concatenate(rows, axis=0).astype(BF16))
+            smooth = dot(ti[...], jnp.concatenate(sides, axis=1))
             smooth = jnp.concatenate([smooth[:, :C], smooth[:, C:]], axis=0)
             noise = nbuf[pl.ds(2 * pair, 2), l].reshape(2 * NX, C)
             pre = dot(jnp.concatenate([smooth.astype(BF16), noise], axis=1), wcat[...])
@@ -299,7 +462,8 @@
             obuf[pl.ds(2 * pair, 2), l] = new.reshape(2, NX, C)
             return carry
         with jax.named_scope("G"):
-            lax.fori_loop(0, nl * NP, column, 0)
+            for l in range(l0, l0 + nl):
+                lax.fori_loop(0, 2, functools.partial(column, l), 0)
 
         def moments(g, carry):
             lats = pl.ds(l0, nl)
@@ -331,15 +495,22 @@
         def _():
             all_bytes(lsend.at[pl.ds(0, NT - 1)], l_ss)
         all_bytes(lrecv.at[pl.ds(0, NG - 1)], k_ss)
-        for b in range(NB):
-            all_bytes(send1.at[b, pl.ds(0, NT - 1)], s1_ss.at[b])
+        all_bytes(qsend.at[pl.ds(0, NY - 1)], q_ss)
+        all_bytes(t1send.at[pl.ds(0, NY - 1)], t1_ss)
+        all_bytes(t3send.at[pl.ds(0, NY - 1)], t3_ss)
+        for k in range(4):
+            all_bytes(rp_send.at[k], rs_ss.at[0, k])
+            all_bytes(fall.at[0], ag_ss.at[0, k])
+            if k < 3:
+                all_bytes(rm_send.at[k], rs_ss.at[1, k])
+                all_bytes(fall.at[0], ag_ss.at[1, k])
+        for pair in range(2):
+            all_bytes(send1.at[pair, pl.ds(0, NT - 1)], s1_ss.at[pair])
+            all_bytes(send2a.at[pair, pl.ds(0, NT - 1)], s2_ss.at[pair])
         for q, (l0, nl) in enumerate(CHUNKS):
             lats = pl.ds(l0, nl)
-            if q == 0:
-                for pair in range(NP):
-                    all_bytes(send2.at[lats, pl.ds(0, NT - 1), pair], s2_ss.at[pair])
-            else:
-                all_bytes(send2.at[lats, pl.ds(0, NT - 1)], s2_ss.at[q + 1])
+            if q > 0:
+                all_bytes(send2b.at[pl.ds(l0 - 2, nl), pl.ds(0, NT - 1)], s2_ss.at[q + 1])
             all_bytes(hrecv.at[lats], h_ss.at[q])
             all_bytes(mrecv.at[lats, pl.ds(0, NX4 - 1)], m_ss.at[q])
             all_bytes(arecv.at[lats, pl.ds(0, NG - 1)], a_ss.at[q])
@@ -371,14 +542,23 @@
             V((H, H), BF16), V((1, H), F32), V((H, H), BF16), V((H, C), BF16),
             V((NT, NX), F32), V((NT, NX), F32), V((2 * C, NX), BF16), V((NX, 2 * C), BF16),
             V((NT, 4 * NL, C), BF16), V((NZ, NY, 4 * NL, C), BF16),
-            V((NB, NT, 48, C), BF16), V((NB, NT, 48, C), BF16),
-            V((NL, NT, NP, 16, C), BF16), V((NL, NT, NP, 16, C), BF16),
-            V((NT * 48, C), F32), V((2, NT * 48, C), F32),
-            V((4, NT * NL, C), BF16), V((4, C, NT * NL), BF16), V((4, C, C), F32),
+            V((NY, NL * NW, C), BF16), V((NY, NL * NW, C), BF16),
+            V((2, NT, NL * 2 * J, C), BF16), V((2, NT, NL * 2 * J, C), BF16),
+            V((2, NT, 4 * J, C), BF16), V((2, NT, 4 * J, C), BF16),
+            V((NL - 2, NT, 4 * J, C), BF16), V((NL - 2, NT, 4 * J, C), BF16),
+            V((NY, 2 * NB, NL * NW, C), BF16), V((NY, 2 * NB, NL * NW, C), BF16),
+            V((NY, 2 * NB, NL * NW, C), BF16), V((NY, 2 * NB, NL * NW, C), BF16),
+            V((NR, NY * NL * NW), BF16), V((NY * NL * NW, NR), BF16), V((NR, C), F32), V((2 * NB, NR, C), F32),
+            V((4, NR, C), BF16), V((4, NR, C), BF16), V((3, NR, C), BF16), V((3, NR, C), BF16), V((NZ, NR, C), BF16),
+            V((NT * NL * 2 * J, C), F32), V((NT * NL * 2 * J, C), F32),
+            V((NL - 2, NT * 4 * J, C), F32), V((NT * 4 * J, C), F32),
+            V((3, NT * NL, C), BF16), V((3, C, NT * NL), BF16), V((3, C, C), F32),
             V((NL, 2, NX4, 2, MX, C), BF16), V((NL, NX4, 2, MX, C), BF16),
             V((NL, NX4, 2, MX, C), BF16), V((NL, NX4, 2, MX, C), BF16),
             V((NL, 2, MX, C), BF16), V((NL, NG, 2, MX, C), BF16),
-            dma((12,)), dma, dma, dma, dma, dma((NB,)), dma((NB,)), dma((NQ + 1,)), dma((NQ + 1,)),
+            dma((12,)), dma, dma, dma, dma, dma, dma, dma, dma, dma, dma,
+            dma((2, 4)), dma((2, 4)), dma((2, 4)), dma((2, 4)),
+            dma((2,)), dma((2,)), dma((NQ + 1,)), dma((NQ + 1,)),
             dma((NQ,)), dma((NQ,)), dma((NQ,)), dma((NQ,)), dma((NQ,)), dma((NQ,)),
         ],
         compiler_params=pltpu.CompilerParams(

time: 101 us -> 105 us (1.040)
  Pallas kernels: 101 us -> 104 us
    pallas_call x1, Pallas kernels: 98.5 us -> 102 us  [per_device(): pl.pallas_call(kernel, out_shape=tuple((V(s, d) for s, d in shapes)), in_...]
where the time goes in v5:
time: 105 us
  Pallas kernels  104 us (99%)
    pallas_call x1, Pallas kernels, per_device(): pl.pallas_call(kernel, out_shape=tuple((V(s, d) for s, d in shapes)), in_...  102 us
    pallas_call x1, Pallas kernels, per_device(): pl.pallas_call(write_out, out_shape=tuple((jax.ShapeDtypeStruct(s, d) for...  2.21 us

profile of v5, /device:TPU:1, one launch (start us, length us, event | category | flops | bytes accessed | tf_op | source)
XLA Modules:
  0.0 104.9 jit_solution(1452951038933953753)
XLA Ops:
  0.6 102.1 %shard_map.112 = (bf16[4,6,384,128]{3,2,1,0:T(8,128)(2,1)S(1)}, f32[6,384,128]{2,1,0:T(8,128)S(1)}, f32[6,384,128]{2,1,0:T(8,128)S(1)}) custom-call(bf16[4,6,384,128]{3,2,1,0:T(8,128)(2,1)} %grid_h.1, bf16[4,6,384,128]{3,2,1,0:T(8,128)(2,1)} %noise_h.1, bf16[6,128,128]{2,1,0:T(8,128)(2,1)} %leg_h.1, f32[1,128]{1,0:T(1,128)} %bitcast.3, ...), custom_call_target="tpu_custom_call" | custom-call | tf_op jit(solution)/shard_map/pallas_call | solution.py:535
  102.7 2.2 %shard_map.113 = (bf16[4,6,384,128]{3,2,1,0:T(8,128)(2,1)}, f32[6,384,128]{2,1,0:T(8,128)}, f32[6,384,128]{2,1,0:T(8,128)}) custom-call(bf16[4,6,384,128]{3,2,1,0:T(8,128)(2,1)S(1)} %get-tuple-element.6.o, f32[6,384,128]{2,1,0:T(8,128)S(1)} %get-tuple-element.7.m, f32[6,384,128]{2,1,0:T(8,128)S(1)} %get-tuple-element.8.v), custom_call_target="tpu_custom_call" | custom-call | tf_op jit(solution)/shard_map/pallas_call | solution.py:569

commit v6 on v5

--- a/solution.py
+++ b/solution.py
@@ -23,15 +23,14 @@
 C = 128
 H = 256
 MX = NX // NG
-CHUNKS = ((0, 2), (2, 2), (4, 1), (5, 1))
+CHUNKS = ((0, 2), (2, 1), (3, 1), (4, 1), (5, 1))
 NQ = len(CHUNKS)
 MATES = ((2, 0), (2, 1), (1, 0), (3, 0), (1, 1), (3, 1), (0, 1))
 LINE = (2, 1, 3)
 J = 6
 NW = 8
-SIZES = (32, 32, 24, 24, 16, 16, 8, 8)
-OFFS = (0, 32, 64, 88, 112, 128, 144, 152)
-NR = 160
+OFFS = (0, 32, 60, 84, 104, 120, 132, 140)
+NR = 144
 
 
 def dot(a, b):
@@ -57,7 +56,7 @@
     for w in range(1, NW):
         wave = wave + jnp.where(col >= OFFS[w], 1, 0)
         start = start + jnp.where(col >= OFFS[w], OFFS[w] - OFFS[w - 1], 0)
-    return wave, col - start + 8 * (wave // 2)
+    return wave, col - start + NY * wave
 
 
 def kernel(
@@ -65,11 +64,11 @@
     obuf, mbuf, vbuf,
     gbuf, nbuf, leg, diff, wcat, bias, wmid, wout, cosa, sina, tf, ti,
     lsend, lrecv, qsend, qrecv, send1, recv1, send2a, recv2a, send2b, recv2b,
-    t1send, t1recv, t3send, t3recv, dmat, dtm, scale3, rf, rp_send, rp_recv, rm_send, rm_recv, fall,
+    t1send, t1recv, t3send, t3recv, dmat, dtm, scale3, rf, rs_send, rs_recv, fall,
     zf, work_a, work_b, work_c, pn, pt, dm,
     msend, hrecv, csend, mrecv, asend, arecv,
-    in_sem, l_ss, l_rs, k_ss, k_rs, q_ss, q_rs, t1_ss, t1_rs, t3_ss, t3_rs, rs_ss, rs_rs, ag_ss, ag_rs,
-    s1_ss, s1_rs, s2_ss, s2_rs, h_ss, h_rs, m_ss, m_rs, a_ss, a_rs,
+    in_sem, l_ss, l_rs, k_ss, k_rs, q_ss, q_rs, t1_ss, t1_rs, t3_ss, t3_rs, rs_ss, rs_rs,
+    s1_ss, s1_rs, s2_ss, s2_rs, h_ss, h_rs, m_ss, m_rs, a_ss, a_rs, b_ss, b_rs,
 ):
     lat, mg = lax.axis_index("lat"), lax.axis_index("grp")
     my, mz = lat // NZ, lax.rem(lat, NZ)
@@ -113,7 +112,10 @@
             src_ref=src, dst_ref=dst, send_sem=ss, recv_sem=rs,
             device_id={"lat": lat_id}, device_id_type=MESH).start()
 
-    up, down = my * NZ + around(1), my * NZ + around(-1)
+    turn = 1 - 2 * mc
+
+    def at(d):
+        return my * NZ + around(turn * d)
 
     loads = [
         (grid_h.at[0], gbuf.at[0]), (grid_h.at[1], gbuf.at[1]), (grid_h.at[2], gbuf.at[2]), (grid_h.at[3], gbuf.at[3]),
@@ -176,10 +178,13 @@
         each_row(dy, lambda t, s: send(
             send1.at[pair, s], recv1.at[pair, me], s1_ss.at[pair], s1_rs.at[pair], t))
 
-    with jax.named_scope("F01"):
+    with jax.named_scope("F"):
         forward(0)
         forward(1)
         pack(0)
+        forward(2)
+        forward(3)
+        pack(1)
     loads[4].wait()
     source = mz == mg
     with jax.named_scope("basis"):
@@ -198,21 +203,18 @@
     with jax.named_scope("barrier"):
         pl.semaphore_wait(barrier, NT - 1 + NG - 1)
 
+    send_first(0, 0)
+    each_y(lambda y, t: send(qsend.at[y], qrecv.at[my], q_ss, q_rs, t))
+    each_y(lambda y, t: send(t1send.at[y], t1recv.at[my], t1_ss, t1_rs, t))
+
     @pl.when(source)
     def _():
         each_peer(lambda t, s: send(lsend.at[s], lrecv.at[mz, my], l_ss, l_rs, t))
         lrecv[mz, my] = lsend[me]
-    send_first(0, 1)
-    each_y(lambda y, t: send(qsend.at[y], qrecv.at[my], q_ss, q_rs, t))
+    send_first(1, 0)
     qrecv[my] = qsend[my]
-    send_first(0, 2)
-    with jax.named_scope("F23"):
-        forward(2)
-        forward(3)
-    each_y(lambda y, t: send(t1send.at[y], t1recv.at[my], t1_ss, t1_rs, t))
     t1recv[my] = t1send[my]
     with jax.named_scope("prep"):
-        pack(1)
         loads[5].wait()
         rows = iota((C, C), 0)
 
@@ -244,39 +246,27 @@
             rf[k] = out[:, :C]
             rf[k + 1] = out[:, C:]
 
-    def reduce_send(k):
-        part = rf[around(4 - k)]
-        if k > 0:
-            part += rp_recv[k - 1].astype(F32)
-        rp_send[k] = part.astype(BF16)
-        if k < 3:
-            part = rf[around(k - 3)]
-            if k > 0:
-                part += rm_recv[k - 1].astype(F32)
-            rm_send[k] = part.astype(BF16)
-        send(rp_send.at[k], rp_recv.at[k], rs_ss.at[0, k], rs_rs.at[0, k], up)
-        if k < 3:
-            send(rm_send.at[k], rm_recv.at[k], rs_ss.at[1, k], rs_rs.at[1, k], down)
-
-    def reduce_wait(k):
-        with jax.named_scope("w_rs"):
-            all_bytes(rp_recv.at[k], rs_rs.at[0, k])
-            if k < 3:
-                all_bytes(rm_recv.at[k], rs_rs.at[1, k])
-
-    def gather_send(k):
-        a, b = around(-k), around(k)
-        send(fall.at[a], fall.at[a], ag_ss.at[0, k], ag_rs.at[0, k], up)
-        if k < 3:
-            send(fall.at[b], fall.at[b], ag_ss.at[1, k], ag_rs.at[1, k], down)
-
-    def gather_wait(k):
-        with jax.named_scope("w_ring"):
-            all_bytes(fall.at[0], ag_rs.at[0, k])
-            if k < 3:
-                all_bytes(fall.at[0], ag_rs.at[1, k])
-
-    reduce_send(0)
+    def ring_send(n, src, dst, hop):
+        send(src, dst, rs_ss.at[n], rs_rs.at[n], at(hop))
+
+    def ring_wait(*ids):
+        for n in ids:
+            all_bytes(fall.at[0], rs_rs.at[n])
+
+    for n, (dest, hop) in enumerate(((4, 2), (3, 1), (-3, -1), (1, 1), (-1, -1))):
+        rs_send[n] = rf[around(turn * dest)].astype(BF16)
+    for n, (dest, hop) in enumerate(((4, 2), (3, 1), (-3, -1), (1, 1), (-1, -1))):
+        ring_send(n, rs_send.at[n], rs_recv.at[n], hop)
+    send_first(0, 1)
+    send_first(0, 2)
+    with jax.named_scope("prep2"):
+        ti[...] = tf[...].astype(F32).T.astype(BF16)
+    with jax.named_scope("w_rsA"):
+        ring_wait(0, 1, 2)
+    rs_send[5] = (rf[around(turn * 2)] + rs_recv[0].astype(F32) + rs_recv[1].astype(F32)).astype(BF16)
+    rs_send[6] = (rf[around(turn * -2)] + rs_recv[2].astype(F32)).astype(BF16)
+    ring_send(5, rs_send.at[5], rs_recv.at[5], 2)
+    ring_send(6, rs_send.at[6], rs_recv.at[6], -2)
     send_first(0, 3)
     with jax.named_scope("w_leg"):
         @pl.when(source)
@@ -289,13 +279,14 @@
     each_mate(lambda g: pltpu.make_async_remote_copy(
         src_ref=lrecv.at[mg], dst_ref=lrecv.at[mg],
         send_sem=k_ss, recv_sem=k_rs, device_id={"grp": g}, device_id_type=MESH).start())
-    reduce_wait(0)
-    reduce_send(1)
-    send_first(0, 0)
-    with jax.named_scope("prep2"):
-        ti[...] = tf[...].astype(F32).T.astype(BF16)
-    reduce_wait(1)
-    reduce_send(2)
+    with jax.named_scope("w_rsB"):
+        ring_wait(3, 4, 5, 6)
+    total = rf[mz]
+    for n in range(3, 7):
+        total += rs_recv[n].astype(F32)
+    fall[mz] = (total * scale3[...]).astype(BF16)
+    for n, hop in enumerate((2, -2, 1, -1)):
+        ring_send(7 + n, fall.at[mz], fall.at[mz], hop)
     send_first(1, 1)
     with jax.named_scope("w_k"):
         all_bytes(lrecv.at[pl.ds(0, NG - 1)], k_rs)
@@ -306,17 +297,6 @@
                 [work_a[pl.ds(4 * l + i, NT, stride=4 * NL), :] for l in range(NL)], axis=0)
             pn[i] = basis.astype(BF16)
             pt[i] = basis.T.astype(BF16)
-    reduce_wait(2)
-    reduce_send(3)
-    send_first(1, 2)
-    reduce_wait(3)
-    total = rf[mz] + rp_recv[3].astype(F32) + rm_recv[2].astype(F32)
-    fall[mz] = (total * scale3[...]).astype(BF16)
-    gather_send(0)
-    send_first(1, 3)
-    gather_wait(0)
-    gather_send(1)
-    send_first(1, 0)
 
     def analyse(pair):
         with jax.named_scope("w_a1"):
@@ -350,27 +330,36 @@
         each_peer(lambda t, s: send(send2a.at[pair, s], recv2a.at[pair, me], s2_ss.at[pair], s2_rs.at[pair], t))
         recv2a[pair, me] = send2a[pair, me]
 
-    gather_wait(1)
-    gather_send(2)
+    with jax.named_scope("w_agA"):
+        ring_wait(7, 8)
+    behind, ahead = around(turn * -2), around(turn * 2)
+    ring_send(11, fall.at[behind], fall.at[behind], 2)
+    ring_send(12, fall.at[behind], fall.at[behind], 1)
+    ring_send(13, fall.at[ahead], fall.at[ahead], -1)
+    send_first(1, 2)
+    send_first(1, 3)
     analyse(0)
-    gather_wait(2)
-    gather_send(3)
     analyse(1)
-    for q in range(1, NQ):
-        l0, nl = CHUNKS[q]
-        lats = pl.ds(l0 - 2, nl)
-        each_peer(lambda t, s: send(
-            send2b.at[lats, s], recv2b.at[lats, me], s2_ss.at[q + 1], s2_rs.at[q + 1], t))
-    for l in range(NL - 2):
-        recv2b[l, me] = send2b[l, me]
-    gather_wait(3)
+    with jax.named_scope("w_agB"):
+        ring_wait(9, 10, 11, 12, 13)
     with jax.named_scope("synth"):
         for k in range(0, 8, 2):
             out = dot(dtm[...], jnp.concatenate([fall[k], fall[k + 1]], axis=1)).astype(BF16)
             t3send[:, k] = out[:, :C].reshape(NY, NL * NW, C)
             t3send[:, k + 1] = out[:, C:].reshape(NY, NL * NW, C)
-    each_y(lambda y, t: send(t3send.at[y], t3recv.at[my], t3_ss, t3_rs, t))
+    for n in range(NL // 2):
+        rows = pl.ds(16 * n, 16)
+        each_y(lambda y, t: send(
+            t3send.at[y, :, rows], t3recv.at[my, :, rows], t3_ss.at[n], t3_rs.at[n], t))
+    with jax.named_scope("s2b"):
+        for q in range(1, NQ):
+            l0, nl = CHUNKS[q]
+            lats = pl.ds(l0 - 2, nl)
+            each_peer(lambda t, s: send(
+                send2b.at[lats, s], recv2b.at[lats, me], s2_ss.at[q + 1], s2_rs.at[q + 1], t))
     t3recv[my] = t3send[my]
+    for l in range(NL - 2):
+        recv2b[l, me] = send2b[l, me]
 
     def join(q):
         l0, nl = CHUNKS[q]
@@ -410,26 +399,38 @@
             square += (2 * NB) * (off * off)
         asend[lats, 0] = mean.astype(BF16)
         asend[lats, 1] = (square * (1.0 / (NB * NG - 1))).astype(BF16)
-        each_mate(lambda g: pltpu.make_async_remote_copy(
-            src_ref=asend.at[lats], dst_ref=arecv.at[lats, mg],
-            send_sem=a_ss.at[q], recv_sem=a_rs.at[q],
-            device_id={"grp": g}, device_id_type=MESH).start())
-        arecv[lats, mg] = asend[lats]
+        for dx in LINE:
+            pltpu.make_async_remote_copy(
+                src_ref=asend.at[lats], dst_ref=arecv.at[lats, mc, mx],
+                send_sem=a_ss.at[q], recv_sem=a_rs.at[q],
+                device_id={"grp": lax.rem(mx + dx, NX4) * 2 + mc}, device_id_type=MESH).start()
+        arecv[lats, mc, mx] = asend[lats]
+
+    def spread(q):
+        l0, nl = CHUNKS[q]
+        lats = pl.ds(l0, nl)
+        with jax.named_scope("w_ag"):
+            all_bytes(mrecv.at[lats, pl.ds(0, NX4 - 1)], a_rs.at[q])
+        pltpu.make_async_remote_copy(
+            src_ref=arecv.at[lats, mc], dst_ref=arecv.at[lats, mc],
+            send_sem=b_ss.at[q], recv_sem=b_rs.at[q],
+            device_id={"grp": mx * 2 + 1 - mc}, device_id_type=MESH).start()
 
     def finish(q):
         l0, nl = CHUNKS[q]
         lats = pl.ds(l0, nl)
-        with jax.named_scope("w_ag"):
-            all_bytes(arecv.at[lats, pl.ds(0, NG - 1)], a_rs.at[q])
+        with jax.named_scope("w_b"):
+            all_bytes(hrecv.at[lats], b_rs.at[q])
         for g in range(NG):
-            mbuf[lats, pl.ds(MX * g, MX), :] = arecv[lats, g, 0].astype(F32)
-            vbuf[lats, pl.ds(MX * g, MX), :] = arecv[lats, g, 1].astype(F32)
+            mbuf[lats, pl.ds(MX * g, MX), :] = arecv[lats, g % 2, g // 2, 0].astype(F32)
+            vbuf[lats, pl.ds(MX * g, MX), :] = arecv[lats, g % 2, g // 2, 1].astype(F32)
 
     for c in loads[6:]:
         c.wait()
-    with jax.named_scope("w_t3"):
-        all_bytes(t3recv.at[pl.ds(0, NY - 1)], t3_rs)
     for q, (l0, nl) in enumerate(CHUNKS):
+        if l0 % 2 == 0:
+            with jax.named_scope("w_t3"):
+                all_bytes(t3recv.at[pl.ds(0, NY - 1), :, pl.ds(8 * l0, 16)], t3_rs.at[l0 // 2])
         with jax.named_scope("w_a2"):
             if q == 0:
                 for pair in range(2):
@@ -486,8 +487,15 @@
         join(q)
         if q >= 1:
             combine(q - 1)
+        if q >= 3:
+            spread(q - 3)
+    spread(NQ - 3)
+    for q in range(NQ - 3):
+        finish(q)
     combine(NQ - 1)
-    for q in range(NQ):
+    spread(NQ - 2)
+    spread(NQ - 1)
+    for q in range(NQ - 3, NQ):
         finish(q)
 
     with jax.named_scope("end"):
@@ -497,13 +505,10 @@
         all_bytes(lrecv.at[pl.ds(0, NG - 1)], k_ss)
         all_bytes(qsend.at[pl.ds(0, NY - 1)], q_ss)
         all_bytes(t1send.at[pl.ds(0, NY - 1)], t1_ss)
-        all_bytes(t3send.at[pl.ds(0, NY - 1)], t3_ss)
-        for k in range(4):
-            all_bytes(rp_send.at[k], rs_ss.at[0, k])
-            all_bytes(fall.at[0], ag_ss.at[0, k])
-            if k < 3:
-                all_bytes(rm_send.at[k], rs_ss.at[1, k])
-                all_bytes(fall.at[0], ag_ss.at[1, k])
+        for n in range(NL // 2):
+            all_bytes(t3send.at[pl.ds(0, NY - 1), :, pl.ds(16 * n, 16)], t3_ss.at[n])
+        for n in range(14):
+            all_bytes(fall.at[0], rs_ss.at[n])
         for pair in range(2):
             all_bytes(send1.at[pair, pl.ds(0, NT - 1)], s1_ss.at[pair])
             all_bytes(send2a.at[pair, pl.ds(0, NT - 1)], s2_ss.at[pair])
@@ -513,12 +518,16 @@
                 all_bytes(send2b.at[pl.ds(l0 - 2, nl), pl.ds(0, NT - 1)], s2_ss.at[q + 1])
             all_bytes(hrecv.at[lats], h_ss.at[q])
             all_bytes(mrecv.at[lats, pl.ds(0, NX4 - 1)], m_ss.at[q])
-            all_bytes(arecv.at[lats, pl.ds(0, NG - 1)], a_ss.at[q])
+            all_bytes(mrecv.at[lats, pl.ds(0, NX4 - 1)], a_ss.at[q])
+            all_bytes(hrecv.at[lats], b_ss.at[q])
 
 
 def write_out(o, m, v, new_h, mean_h, var_h, sem):
-    copies = [pltpu.make_async_copy(s, d, sem.at[n])
-              for n, (s, d) in enumerate(((o, new_h), (m, mean_h), (v, var_h)))]
+    pieces = [(o.at[b], new_h.at[b]) for b in range(NB)]
+    for n in range(2):
+        half = pl.ds(n * (NL // 2), NL // 2)
+        pieces += [(m.at[half], mean_h.at[half]), (v.at[half], var_h.at[half])]
+    copies = [pltpu.make_async_copy(s, d, sem.at[n]) for n, (s, d) in enumerate(pieces)]
     for c in copies:
         c.start()
     for c in copies:
@@ -549,17 +558,17 @@
             V((NY, 2 * NB, NL * NW, C), BF16), V((NY, 2 * NB, NL * NW, C), BF16),
             V((NY, 2 * NB, NL * NW, C), BF16), V((NY, 2 * NB, NL * NW, C), BF16),
             V((NR, NY * NL * NW), BF16), V((NY * NL * NW, NR), BF16), V((NR, C), F32), V((2 * NB, NR, C), F32),
-            V((4, NR, C), BF16), V((4, NR, C), BF16), V((3, NR, C), BF16), V((3, NR, C), BF16), V((NZ, NR, C), BF16),
+            V((7, NR, C), BF16), V((7, NR, C), BF16), V((NZ, NR, C), BF16),
             V((NT * NL * 2 * J, C), F32), V((NT * NL * 2 * J, C), F32),
             V((NL - 2, NT * 4 * J, C), F32), V((NT * 4 * J, C), F32),
             V((3, NT * NL, C), BF16), V((3, C, NT * NL), BF16), V((3, C, C), F32),
             V((NL, 2, NX4, 2, MX, C), BF16), V((NL, NX4, 2, MX, C), BF16),
             V((NL, NX4, 2, MX, C), BF16), V((NL, NX4, 2, MX, C), BF16),
-            V((NL, 2, MX, C), BF16), V((NL, NG, 2, MX, C), BF16),
-            dma((12,)), dma, dma, dma, dma, dma, dma, dma, dma, dma, dma,
-            dma((2, 4)), dma((2, 4)), dma((2, 4)), dma((2, 4)),
+            V((NL, 2, MX, C), BF16), V((NL, 2, NX4, 2, MX, C), BF16),
+            dma((12,)), dma, dma, dma, dma, dma, dma, dma, dma, dma((NL // 2,)), dma((NL // 2,)),
+            dma((14,)), dma((14,)),
             dma((2,)), dma((2,)), dma((NQ + 1,)), dma((NQ + 1,)),
-            dma((NQ,)), dma((NQ,)), dma((NQ,)), dma((NQ,)), dma((NQ,)), dma((NQ,)),
+            dma((NQ,)), dma((NQ,)), dma((NQ,)), dma((NQ,)), dma((NQ,)), dma((NQ,)), dma((NQ,)), dma((NQ,)),
         ],
         compiler_params=pltpu.CompilerParams(
             collective_id=0, has_side_effects=True, vmem_limit_bytes=48 * 1024 * 1024),
@@ -571,7 +580,7 @@
         out_shape=tuple(jax.ShapeDtypeStruct(s, d) for s, d in shapes),
         in_specs=[vm] * 3,
         out_specs=(hbm,) * 3,
-        scratch_shapes=[dma((3,))],
+        scratch_shapes=[dma((8,))],
         compiler_params=pltpu.CompilerParams(vmem_limit_bytes=1024 * 1024),
     )(*[pltpu.with_memory_space_constraint(a, pltpu.VMEM) for a in held])
 

time: 105 us -> 94 us (0.90)
  Pallas kernels: 104 us -> 93.3 us
    pallas_call x1, Pallas kernels: 102 us -> 91.1 us  [per_device(): pl.pallas_call(kernel, out_shape=tuple((V(s, d) for s, d in shapes)), in_...]
where the time goes in v6:
time: 94 us; the launch traced here: 93.9 us
  Pallas kernels  93.3 us (99%)
    pallas_call x1, Pallas kernels, per_device(): pl.pallas_call(kernel, out_shape=tuple((V(s, d) for s, d in shapes)), in_...  91.1 us
    pallas_call x1, Pallas kernels, per_device(): pl.pallas_call(write_out, out_shape=tuple((jax.ShapeDtypeStruct(s, d) for...  2.25 us

profile of v6, /device:TPU:1, one launch (start us, length us, event | category | flops | bytes accessed | tf_op | source)
XLA Modules:
  0.0 93.9 jit_solution(4546216385978531641)
XLA Ops:
  0.6 91.1 %shard_map.112 = (bf16[4,6,384,128]{3,2,1,0:T(8,128)(2,1)S(1)}, f32[6,384,128]{2,1,0:T(8,128)S(1)}, f32[6,384,128]{2,1,0:T(8,128)S(1)}) custom-call(bf16[4,6,384,128]{3,2,1,0:T(8,128)(2,1)} %grid_h.1, bf16[4,6,384,128]{3,2,1,0:T(8,128)(2,1)} %noise_h.1, bf16[6,128,128]{2,1,0:T(8,128)(2,1)} %leg_h.1, f32[1,128]{1,0:T(1,128)} %bitcast.3, ...), custom_call_target="tpu_custom_call" | custom-call | tf_op jit(solution)/shard_map/pallas_call | solution.py:544
  91.7 2.2 %shard_map.113 = (bf16[4,6,384,128]{3,2,1,0:T(8,128)(2,1)}, f32[6,384,128]{2,1,0:T(8,128)}, f32[6,384,128]{2,1,0:T(8,128)}) custom-call(bf16[4,6,384,128]{3,2,1,0:T(8,128)(2,1)S(1)} %get-tuple-element.6.o, f32[6,384,128]{2,1,0:T(8,128)S(1)} %get-tuple-element.7.m, f32[6,384,128]{2,1,0:T(8,128)S(1)} %get-tuple-element.8.v), custom_call_target="tpu_custom_call" | custom-call | tf_op jit(solution)/shard_map/pallas_call | solution.py:578

commit v7 on v6

--- a/solution.py
+++ b/solution.py
@@ -1,4 +1,3 @@
-import functools
 import math
 
 import jax
@@ -438,16 +437,17 @@
             else:
                 all_bytes(recv2b.at[pl.ds(l0 - 2, nl), pl.ds(0, NT - 1)], s2_rs.at[q + 1])
 
-        def column(l, pair, carry):
+        def column(l, pair):
+            area = work_a.at[pl.ds(pair * NT * 4 * J, NT * 4 * J)]
             if l < 2:
-                work_c[...] = recv2a[pair].astype(F32).reshape(NT * 4 * J, C)
+                area[...] = recv2a[pair].astype(F32).reshape(NT * 4 * J, C)
                 first = 2 * J * l
             else:
-                work_c[...] = recv2b[l - 2].astype(F32).reshape(NT * 4 * J, C)
+                area[...] = recv2b[l - 2].astype(F32).reshape(NT * 4 * J, C)
                 first = 2 * J * pair
             sides = []
             for k in range(2):
-                rows = [work_c[pl.ds(first + J * k + j, NT, stride=4 * J), :] for j in range(J)]
+                rows = [area[pl.ds(first + J * k + j, NT, stride=4 * J), :] for j in range(J)]
                 for y in range(NY):
                     for r in range(2):
                         two = t3recv[y, r * NB + 2 * pair + k, pl.ds(16 * (l // 2), 16), :].astype(F32)
@@ -461,10 +461,10 @@
             two = silu(dot(one, wmid[...])).astype(BF16)
             new = (smooth + dot(two, wout[...])).astype(BF16)
             obuf[pl.ds(2 * pair, 2), l] = new.reshape(2, NX, C)
-            return carry
         with jax.named_scope("G"):
             for l in range(l0, l0 + nl):
-                lax.fori_loop(0, 2, functools.partial(column, l), 0)
+                for pair in range(2):
+                    column(l, pair)
 
         def moments(g, carry):
             lats = pl.ds(l0, nl)
@@ -484,17 +484,21 @@
             src_ref=msend.at[lats, 1 - mc], dst_ref=hrecv.at[lats],
             send_sem=h_ss.at[q], recv_sem=h_rs.at[q],
             device_id={"grp": mx * 2 + 1 - mc}, device_id_type=MESH).start()
-        join(q)
-        if q >= 1:
-            combine(q - 1)
-        if q >= 3:
-            spread(q - 3)
-    spread(NQ - 3)
+        if 1 <= q < NQ - 1:
+            join(q - 1)
+        if 2 <= q < NQ - 1:
+            combine(q - 2)
+        if q >= NQ - 2:
+            join(q)
+    combine(NQ - 3)
+    for q in range(NQ - 3):
+        spread(q)
     for q in range(NQ - 3):
         finish(q)
+    combine(NQ - 2)
     combine(NQ - 1)
-    spread(NQ - 2)
-    spread(NQ - 1)
+    for q in range(NQ - 3, NQ):
+        spread(q)
     for q in range(NQ - 3, NQ):
         finish(q)
 

time: 94 us -> 91.9 us (0.978)
  Pallas kernels: 93.3 us -> 91.2 us
    pallas_call x1, Pallas kernels: 91.1 us -> 88.9 us  [per_device(): pl.pallas_call(kernel, out_shape=tuple((V(s, d) for s, d in shapes)), in_...]
where the time goes in v7:
time: 91.9 us; the launch traced here: 91.8 us
  Pallas kernels  91.2 us (99%)
    pallas_call x1, Pallas kernels, per_device(): pl.pallas_call(kernel, out_shape=tuple((V(s, d) for s, d in shapes)), in_...  88.9 us
    pallas_call x1, Pallas kernels, per_device(): pl.pallas_call(write_out, out_shape=tuple((jax.ShapeDtypeStruct(s, d) for...  2.25 us

profile of v7, /device:TPU:1, one launch (start us, length us, event | category | flops | bytes accessed | tf_op | source)
XLA Modules:
  0.0 91.8 jit_solution(2205332711822610163)
XLA Ops:
  0.6 88.9 %shard_map.112 = (bf16[4,6,384,128]{3,2,1,0:T(8,128)(2,1)S(1)}, f32[6,384,128]{2,1,0:T(8,128)S(1)}, f32[6,384,128]{2,1,0:T(8,128)S(1)}) custom-call(bf16[4,6,384,128]{3,2,1,0:T(8,128)(2,1)} %grid_h.1, bf16[4,6,384,128]{3,2,1,0:T(8,128)(2,1)} %noise_h.1, bf16[6,128,128]{2,1,0:T(8,128)(2,1)} %leg_h.1, f32[1,128]{1,0:T(1,128)} %bitcast.3, ...), custom_call_target="tpu_custom_call" | custom-call | tf_op jit(solution)/shard_map/pallas_call | solution.py:548
  89.6 2.2 %shard_map.113 = (bf16[4,6,384,128]{3,2,1,0:T(8,128)(2,1)}, f32[6,384,128]{2,1,0:T(8,128)}, f32[6,384,128]{2,1,0:T(8,128)}) custom-call(bf16[4,6,384,128]{3,2,1,0:T(8,128)(2,1)S(1)} %get-tuple-element.6.o, f32[6,384,128]{2,1,0:T(8,128)S(1)} %get-tuple-element.7.m, f32[6,384,128]{2,1,0:T(8,128)S(1)} %get-tuple-element.8.v), custom_call_target="tpu_custom_call" | custom-call | tf_op jit(solution)/shard_map/pallas_call | solution.py:582

commit v8 on v7

--- a/solution.py
+++ b/solution.py
@@ -211,6 +211,7 @@
         each_peer(lambda t, s: send(lsend.at[s], lrecv.at[mz, my], l_ss, l_rs, t))
         lrecv[mz, my] = lsend[me]
     send_first(1, 0)
+    send_first(0, 1)
     qrecv[my] = qsend[my]
     t1recv[my] = t1send[my]
     with jax.named_scope("prep"):
@@ -252,21 +253,29 @@
         for n in ids:
             all_bytes(fall.at[0], rs_rs.at[n])
 
-    for n, (dest, hop) in enumerate(((4, 2), (3, 1), (-3, -1), (1, 1), (-1, -1))):
+    first = ((4, 2), (3, 1), (-3, -1))
+    for n, (dest, hop) in enumerate(first):
         rs_send[n] = rf[around(turn * dest)].astype(BF16)
-    for n, (dest, hop) in enumerate(((4, 2), (3, 1), (-3, -1), (1, 1), (-1, -1))):
+    for n, (dest, hop) in enumerate(first):
         ring_send(n, rs_send.at[n], rs_recv.at[n], hop)
-    send_first(0, 1)
     send_first(0, 2)
     with jax.named_scope("prep2"):
         ti[...] = tf[...].astype(F32).T.astype(BF16)
     with jax.named_scope("w_rsA"):
         ring_wait(0, 1, 2)
-    rs_send[5] = (rf[around(turn * 2)] + rs_recv[0].astype(F32) + rs_recv[1].astype(F32)).astype(BF16)
-    rs_send[6] = (rf[around(turn * -2)] + rs_recv[2].astype(F32)).astype(BF16)
-    ring_send(5, rs_send.at[5], rs_recv.at[5], 2)
-    ring_send(6, rs_send.at[6], rs_recv.at[6], -2)
+    rs_send[3] = (rf[around(turn * 2)] + rs_recv[0].astype(F32) + rs_recv[1].astype(F32)).astype(BF16)
+    rs_send[4] = (rf[around(turn * -2)] + rs_recv[2].astype(F32)).astype(BF16)
+    ring_send(3, rs_send.at[3], rs_recv.at[3], 1)
+    ring_send(4, rs_send.at[4], rs_recv.at[4], -1)
     send_first(0, 3)
+    send_first(1, 1)
+    with jax.named_scope("w_rsB"):
+        ring_wait(3, 4)
+    rs_send[5] = (rf[around(turn)] + rs_recv[3].astype(F32)).astype(BF16)
+    rs_send[6] = (rf[around(-turn)] + rs_recv[4].astype(F32)).astype(BF16)
+    ring_send(5, rs_send.at[5], rs_recv.at[5], 1)
+    ring_send(6, rs_send.at[6], rs_recv.at[6], -1)
+    send_first(1, 2)
     with jax.named_scope("w_leg"):
         @pl.when(source)
         def _():
@@ -278,15 +287,13 @@
     each_mate(lambda g: pltpu.make_async_remote_copy(
         src_ref=lrecv.at[mg], dst_ref=lrecv.at[mg],
         send_sem=k_ss, recv_sem=k_rs, device_id={"grp": g}, device_id_type=MESH).start())
-    with jax.named_scope("w_rsB"):
-        ring_wait(3, 4, 5, 6)
-    total = rf[mz]
-    for n in range(3, 7):
-        total += rs_recv[n].astype(F32)
+    with jax.named_scope("w_rsC"):
+        ring_wait(5, 6)
+    total = rf[mz] + rs_recv[5].astype(F32) + rs_recv[6].astype(F32)
     fall[mz] = (total * scale3[...]).astype(BF16)
-    for n, hop in enumerate((2, -2, 1, -1)):
-        ring_send(7 + n, fall.at[mz], fall.at[mz], hop)
-    send_first(1, 1)
+    ring_send(7, fall.at[mz], fall.at[mz], 1)
+    ring_send(8, fall.at[mz], fall.at[mz], -1)
+    send_first(1, 3)
     with jax.named_scope("w_k"):
         all_bytes(lrecv.at[pl.ds(0, NG - 1)], k_rs)
     with jax.named_scope("prepP"):
@@ -331,16 +338,18 @@
 
     with jax.named_scope("w_agA"):
         ring_wait(7, 8)
-    behind, ahead = around(turn * -2), around(turn * 2)
-    ring_send(11, fall.at[behind], fall.at[behind], 2)
-    ring_send(12, fall.at[behind], fall.at[behind], 1)
-    ring_send(13, fall.at[ahead], fall.at[ahead], -1)
-    send_first(1, 2)
-    send_first(1, 3)
+    for n, side in ((9, -1), (10, 1)):
+        near = around(turn * side)
+        ring_send(n, fall.at[near], fall.at[near], -side)
     analyse(0)
+    with jax.named_scope("w_agB"):
+        ring_wait(9, 10)
+    for n, side, hop in ((12, -2, 2), (11, -2, 1), (13, 2, -1)):
+        far = around(turn * side)
+        ring_send(n, fall.at[far], fall.at[far], hop)
     analyse(1)
-    with jax.named_scope("w_agB"):
-        ring_wait(9, 10, 11, 12, 13)
+    with jax.named_scope("w_agC"):
+        ring_wait(11, 12, 13)
     with jax.named_scope("synth"):
         for k in range(0, 8, 2):
             out = dot(dtm[...], jnp.concatenate([fall[k], fall[k + 1]], axis=1)).astype(BF16)

time: 91.9 us -> 89.8 us (0.977)
  Pallas kernels: 91.2 us -> 89.1 us
    pallas_call x1, Pallas kernels: 88.9 us -> 86.8 us  [per_device(): pl.pallas_call(kernel, out_shape=tuple((V(s, d) for s, d in shapes)), in_...]
where the time goes in v8:
time: 89.8 us; the launch traced here: 89.7 us
  Pallas kernels  89.1 us (99%)
    pallas_call x1, Pallas kernels, per_device(): pl.pallas_call(kernel, out_shape=tuple((V(s, d) for s, d in shapes)), in_...  86.8 us
    pallas_call x1, Pallas kernels, per_device(): pl.pallas_call(write_out, out_shape=tuple((jax.ShapeDtypeStruct(s, d) for...  2.25 us

profile of v8, /device:TPU:1, one launch (start us, length us, event | category | flops | bytes accessed | tf_op | source)
XLA Modules:
  0.0 89.7 jit_solution(2704630573681258233)
XLA Ops:
  0.6 86.8 %shard_map.112 = (bf16[4,6,384,128]{3,2,1,0:T(8,128)(2,1)S(1)}, f32[6,384,128]{2,1,0:T(8,128)S(1)}, f32[6,384,128]{2,1,0:T(8,128)S(1)}) custom-call(bf16[4,6,384,128]{3,2,1,0:T(8,128)(2,1)} %grid_h.1, bf16[4,6,384,128]{3,2,1,0:T(8,128)(2,1)} %noise_h.1, bf16[6,128,128]{2,1,0:T(8,128)(2,1)} %leg_h.1, f32[1,128]{1,0:T(1,128)} %bitcast.3, ...), custom_call_target="tpu_custom_call" | custom-call | tf_op jit(solution)/shard_map/pallas_call | solution.py:557
  87.5 2.2 %shard_map.113 = (bf16[4,6,384,128]{3,2,1,0:T(8,128)(2,1)}, f32[6,384,128]{2,1,0:T(8,128)}, f32[6,384,128]{2,1,0:T(8,128)}) custom-call(bf16[4,6,384,128]{3,2,1,0:T(8,128)(2,1)S(1)} %get-tuple-element.6.o, f32[6,384,128]{2,1,0:T(8,128)S(1)} %get-tuple-element.7.m, f32[6,384,128]{2,1,0:T(8,128)S(1)} %get-tuple-element.8.v), custom_call_target="tpu_custom_call" | custom-call | tf_op jit(solution)/shard_map/pallas_call | solution.py:591
